TPU v7x, 32 devices: a whole 2x2x4 slice. The times are simulated.
32 devices in a mesh: grp: 4 (over z), shard: 8 (over y, x, core).
Axes of the slice: x: 2, y: 2, z: 4, core: 2. Of those that a mesh axis runs over, the one named last changes fastest.
Arguments:
- partial_grads: bfloat16 [4, 4096, 6144], P('grp', 'shard')
- joined_block: int32 [48], replicated, may hold values from 0 to 47, each once
- head_slot: int32 [48], replicated, may hold values from 0 to 47, as said below
Outputs:
- head_grads: float32 [48, 8, 512, 128], P('shard', None, 'grp')
- head_rms: float32 [48], P('shard')
- type_rms: float32 [3], replicated
Inputs may be any that keep to these rules, and one draw needn't show every extreme that they name: `joined_block`: a permutation: each block number appears once. `head_slot`: distinct slots; every owner along shard holds 6 or 5 head blocks, and some owner holds 6.
All inputs are finite; a program needn't handle non-finite values.
Results may differ from a plain program's by a relative error of at most 0.0003.
Values may be sent and summed in bfloat16 or wider, within the bound.
A program may use at most 64 MiB of HBM per device.

v0:
```python
import functools

import jax
import jax.numpy as jnp
from jax import lax
from jax.experimental import pallas as pl
from jax.experimental.pallas import tpu as pltpu
from jax.sharding import PartitionSpec as P

D = 4096
QH = 32
KVH = 8
HS = 128
LANES = 128
MESH = pl.DeviceIdType.MESH


def chunk_rows(rows):
    return 16 if rows % 16 == 0 else rows


QMAX = 8388600.0
TINY = 2.0**-126
AHEAD = 3


def pack(pair):
    peaks, codes = [], []
    for tile in pair:
        peak = jnp.max(jnp.abs(tile), axis=(0, 1), keepdims=True)
        shrink = jnp.where(peak > 2.0**100, 2.0**-24, 1.0)
        scale = 1.0 / jnp.maximum(peak * shrink, TINY)
        code = jnp.round(tile * shrink * scale * QMAX).astype(jnp.int32)
        peaks.append(peak)
        codes += [code[:8], code[8:]]
    a, b, c, d = codes
    words = (
        (a << 8) | (d & 255),
        (b << 8) | ((d >> 8) & 255),
        (c << 8) | ((d >> 16) & 255),
    )
    return words, peaks


def unpack(words):
    a, b, c = words
    d = (a & 255) | ((b & 255) << 8) | ((c << 24) >> 8)
    return [
        jnp.concatenate([lo.astype(jnp.float32), hi.astype(jnp.float32)], axis=0) * (1.0 / QMAX)
        for lo, hi in ((a >> 8, b >> 8), (c >> 8, d))
    ]


def kernel(groups, shards, blocks, slots_dev, chunks, relay, *refs):
    x_ref, joined_ref, slot_ref = refs[:3]
    out_ref, head_ref, type_ref = refs[3:6]
    own = refs[6]
    got = refs[7 : 7 + chunks]
    ready = refs[7 + chunks : 7 + 2 * chunks]
    rest = refs[7 + 2 * chunks :]
    if relay:
        far, passed, out_words, out_peaks, in_words, in_peaks, plain = rest[-14:-7]
        far_sem, r_send, r_recv, p_send, p_recv, d_send, d_recv = rest[-7:]
        rest = rest[:-14]
    (source, taken, kind_of, summed, squares, shard_part, shard_all, grp_part, grp_all) = rest[:9]
    (own_sem, z_send, z_recv, a_send, a_recv, keep_sem, s_send, s_recv, g_send, g_recv) = rest[9:]

    grp = lax.axis_index("grp")
    shard = lax.axis_index("shard")
    slots = slots_dev * shards
    rows = own.shape[0]
    part = rows // chunks
    width = own.shape[1] // blocks

    def grp_peer(offset):
        return lax.rem(grp + offset, groups)

    def shard_peer(offset):
        return lax.rem(shard + offset, shards)

    load_own = pltpu.make_async_copy(
        x_ref.at[0, pl.ds(pl.multiple_of(grp * rows, 8), rows), :], own, own_sem
    )
    load_own.start()

    barrier = pltpu.get_barrier_semaphore()
    for o in range(1, groups):
        pl.semaphore_signal(barrier, 1, device_id=(grp_peer(o), shard), device_id_type=MESH)
    for o in range(1, shards):
        pl.semaphore_signal(barrier, 1, device_id=(grp, shard_peer(o)), device_id_type=MESH)
    pl.semaphore_wait(barrier, groups + shards - 2)

    z_copies = []
    if relay:
        outer = (grp == 0) | (grp == groups - 1)
        inner = jnp.logical_not(outer)
        mate = grp + 1 - 2 * lax.rem(grp, 2)
        near = jnp.where(outer, 3 - mate, 3 - grp)
        dests = (near, near + 1 - 2 * lax.rem(near, 2))

        def rows_of(dest, c):
            return x_ref.at[0, pl.ds(pl.multiple_of(dest * rows + c * part, 8), part), :]

        def far_copy(f):
            first = pl.multiple_of(dests[f] * rows, 8)
            return pltpu.make_async_copy(x_ref.at[0, pl.ds(first, rows), :], far.at[f], far_sem.at[f])

        def relay_copy(c, f):
            return pltpu.make_async_remote_copy(
                src_ref=rows_of(dests[f], c),
                dst_ref=passed.at[c, f],
                send_sem=r_send.at[c, f],
                recv_sem=r_recv.at[c, f],
                device_id=(mate, shard),
                device_id_type=MESH,
            )

        def mate_copy(c):
            return pltpu.make_async_remote_copy(
                src_ref=rows_of(mate, c),
                dst_ref=got[c].at[0],
                send_sem=z_send.at[c, 0],
                recv_sem=z_recv.at[c, 0],
                device_id=(mate, shard),
                device_id_type=MESH,
            )

        def packed_copies(c, f):
            return [
                pltpu.make_async_remote_copy(
                    src_ref=src.at[c, f],
                    dst_ref=dst.at[c],
                    send_sem=p_send.at[c, f, i],
                    recv_sem=p_recv.at[c, i],
                    device_id=(dests[f], shard),
                    device_id_type=MESH,
                )
                for i, (src, dst) in enumerate(((out_words, in_words), (out_peaks, in_peaks)))
            ]

        def plain_copy(f, place):
            return pltpu.make_async_remote_copy(
                src_ref=rows_of(dests[f], 0),
                dst_ref=plain.at[place],
                send_sem=d_send.at[f],
                recv_sem=d_recv.at[place],
                device_id=(dests[f], shard),
                device_id_type=MESH,
            )

        def pack_chunk(c):
            mate_copy(c).start()
            for f in range(2):
                relay_copy(c, f).wait_recv()

                def pack_pair(p, peaks, f=f):
                    at = pl.multiple_of(p * 2 * width, 2 * width)
                    pair = far[f, c * part : (c + 1) * part, pl.ds(at, 2 * width)].astype(jnp.float32)
                    pair += passed[c, f, :, pl.ds(at, 2 * width)].astype(jnp.float32)
                    words, tops = pack((pair[:, :width], pair[:, width:]))
                    for i in range(3):
                        out_words[c, f, p, i] = words[i]
                    lane = lax.broadcasted_iota(jnp.int32, (1, LANES), 1)
                    peaks = jnp.where(lane == 2 * p, tops[0], peaks)
                    return jnp.where(lane == 2 * p + 1, tops[1], peaks)

                out_peaks[c, f] = lax.fori_loop(
                    0, blocks // 2, pack_pair, jnp.zeros((1, LANES), jnp.float32), unroll=4
                )
                for copy in packed_copies(c, f):
                    copy.start()

        for f in range(2):
            plain_copy(f, jnp.where(outer, 1, 0)).start()

        @pl.when(outer)
        def _():
            for c in range(1, chunks):
                for f in range(2):
                    relay_copy(c, f).start()
                if c >= AHEAD:
                    mate_copy(c - AHEAD).start()
            for c in range(max(chunks - AHEAD, 0), chunks):
                mate_copy(c).start()

        @pl.when(inner)
        def _():
            mate_copy(0).start()

        for f in range(2):
            far_copy(f).start()
    else:
        for c in range(chunks):
            for o in range(1, groups):
                first = pl.multiple_of(grp_peer(o) * rows + c * part, 8)
                copy = pltpu.make_async_remote_copy(
                    src_ref=x_ref.at[0, pl.ds(first, part), :],
                    dst_ref=got[c].at[o - 1],
                    send_sem=z_send.at[c, o - 1],
                    recv_sem=z_recv.at[c, o - 1],
                    device_id=(grp_peer(o), shard),
                    device_id_type=MESH,
                )
                copy.start()
                z_copies.append(copy)

    def find(j, carry):
        found, block, kind = jnp.float32(0), jnp.int32(0), jnp.int32(3)
        for b in range(blocks):
            hit = slot_ref[b] == j
            found = jnp.where(hit, 1.0, found)
            block = jnp.where(hit, joined_ref[b], block)
            kind = jnp.where(hit, (b >= QH) + (b >= QH + KVH), kind)
        source[j] = block
        taken[j] = found
        kind_of[j] = kind
        return carry

    lax.fori_loop(0, slots, find, 0)

    load_own.wait()
    if relay:
        for f in range(2):
            far_copy(f).wait()
    a_copies = []
    for step in range(chunks + AHEAD if relay else chunks):
        if relay and 0 < step < chunks:
            pl.when(inner)(functools.partial(pack_chunk, step))
        c = step - AHEAD if relay else step
        if c < 0:
            continue
        if relay:
            mate_copy(c).wait_recv()
            if c == 0:
                for place in range(2):
                    plain_copy(0, place).wait_recv()
            else:
                for copy in packed_copies(c, 0):
                    copy.wait_recv()
                peaks = in_peaks[c]

            def add_pair(p, carry):
                at = pl.multiple_of(p * 2 * width, 2 * width)
                pair = own[c * part : (c + 1) * part, pl.ds(at, 2 * width)].astype(jnp.float32)
                pair += got[c][0, :, pl.ds(at, 2 * width)].astype(jnp.float32)
                if c == 0:
                    for place in range(2):
                        pair += plain[place, :, pl.ds(at, 2 * width)].astype(jnp.float32)
                    for h in range(2):
                        summed[2 * p + h] = pair[:, h * width : (h + 1) * width]
                    return carry
                tiles = unpack([in_words[c, p, i] for i in range(3)])
                lane = lax.broadcasted_iota(jnp.int32, (1, LANES), 1)
                for h in range(2):
                    peak = jnp.sum(jnp.where(lane == 2 * p + h, peaks, 0.0), axis=1, keepdims=True)
                    summed[2 * p + h] = pair[:, h * width : (h + 1) * width] + tiles[h] * peak
                return carry

            lax.fori_loop(0, blocks // 2, add_pair, 0, unroll=4)
        else:
            for o in range(1, groups):
                z_copies[c * (groups - 1) + o - 1].wait_recv()

            def add(k, carry):
                at = pl.multiple_of(k * width, width)
                total = own[c * part : (c + 1) * part, pl.ds(at, width)].astype(jnp.float32)
                for o in range(1, groups):
                    total += got[c][o - 1, :, pl.ds(at, width)].astype(jnp.float32)
                summed[k] = total
                return carry

            lax.fori_loop(0, blocks, add, 0, unroll=4)

        def slot(j, carry):
            total = summed[source[j]] * taken[j]
            ready[c][j] = total
            sq = jnp.sum((total * total).reshape(part // 8, 8, width), axis=0)
            squares[j] = sq if c == 0 else squares[j] + sq
            return carry

        lax.fori_loop(0, slots, slot, 0, unroll=4)

        if c == chunks - 1:
            lane = lax.broadcasted_iota(jnp.int32, (slots, LANES), 1)
            row = lax.broadcasted_iota(jnp.int32, (slots, LANES), 0)
            per_slot = jnp.sum(jnp.sum(squares[...], axis=1), axis=1, keepdims=True)
            shard_part[...] = jnp.sum(jnp.where(lane == row, per_slot, 0.0), axis=0, keepdims=True)
            s_copies = []
            for o in range(1, shards):
                copy = pltpu.make_async_remote_copy(
                    src_ref=shard_part,
                    dst_ref=shard_all.at[o - 1],
                    send_sem=s_send.at[o - 1],
                    recv_sem=s_recv.at[o - 1],
                    device_id=(grp, shard_peer(o)),
                    device_id_type=MESH,
                )
                copy.start()
                s_copies.append(copy)

        for o in range(1, shards):
            copy = pltpu.make_async_remote_copy(
                src_ref=ready[c].at[pl.ds(shard_peer(o) * slots_dev, slots_dev)],
                dst_ref=out_ref.at[:, shard, pl.ds(c * part, part), :],
                send_sem=a_send.at[c, o - 1],
                recv_sem=a_recv.at[c, o - 1],
                device_id=(grp, shard_peer(o)),
                device_id_type=MESH,
            )
            copy.start()
            a_copies.append(copy)
        copy = pltpu.make_async_copy(
            ready[c].at[pl.ds(shard * slots_dev, slots_dev)],
            out_ref.at[:, shard, pl.ds(c * part, part), :],
            keep_sem.at[c],
        )
        copy.start()
        a_copies.append(copy)

    total = shard_part[...]
    for o in range(1, shards):
        s_copies[o - 1].wait()
        total = total + shard_all[o - 1]
    grp_part[...] = total
    g_copies = []
    for o in range(1, groups):
        copy = pltpu.make_async_remote_copy(
            src_ref=grp_part,
            dst_ref=grp_all.at[o - 1],
            send_sem=g_send.at[o - 1],
            recv_sem=g_recv.at[o - 1],
            device_id=(grp_peer(o), shard),
            device_id_type=MESH,
        )
        copy.start()
        g_copies.append(copy)
    lane = lax.broadcasted_iota(jnp.int32, (1, LANES), 1)

    def lay(j, kinds):
        return jnp.where(lane == j, kind_of[j], kinds)

    kinds = lax.fori_loop(0, slots, lay, jnp.full((1, LANES), 3, jnp.int32))
    for o in range(1, groups):
        g_copies[o - 1].wait()
        total = total + grp_all[o - 1]
    root = jnp.sqrt(total / (D * HS))
    for i in range(slots_dev):
        head_ref[i] = jnp.sum(jnp.where(lane == shard * slots_dev + i, root, 0.0))
    for t, heads in enumerate((QH, KVH, KVH)):
        one = jnp.sum(jnp.where(kinds == t, total, 0.0), axis=1, keepdims=True)
        type_ref[t] = jnp.sum(jnp.sqrt(one / (heads * D * HS)))

    if relay:
        for c in range(chunks):
            mate_copy(c).wait_send()
        for f in range(2):
            plain_copy(f, 0).wait_send()

        @pl.when(outer)
        def _():
            for c in range(1, chunks):
                for f in range(2):
                    relay_copy(c, f).wait_send()

        @pl.when(inner)
        def _():
            for c in range(1, chunks):
                for f in range(2):
                    for copy in packed_copies(c, f):
                        copy.wait_send()

    for copy in z_copies:
        copy.wait_send()
    for copy in a_copies:
        copy.wait()


def solution(mesh):
    groups, shards = mesh.shape["grp"], mesh.shape["shard"]

    def step(x, joined, slot):
        blocks = joined.shape[0]
        slots_dev = (blocks + shards - 1) // shards
        slots = slots_dev * shards
        rows = x.shape[1] // groups
        cols = x.shape[2]
        width = cols // blocks
        part = chunk_rows(rows)
        chunks = rows // part
        dma = pltpu.SemaphoreType.DMA
        relay = groups == 4 and part == 16 and blocks % 2 == 0 and blocks <= LANES
        relay = relay and width == LANES
        arrivals = 1 if relay else groups - 1
        return tuple(
            pl.pallas_call(
                functools.partial(kernel, groups, shards, blocks, slots_dev, chunks, relay),
                out_shape=[
                    jax.ShapeDtypeStruct((slots_dev, shards, rows, width), jnp.float32),
                    jax.ShapeDtypeStruct((slots_dev,), jnp.float32),
                    jax.ShapeDtypeStruct((3,), jnp.float32),
                ],
                in_specs=[
                    pl.BlockSpec(memory_space=pltpu.HBM),
                    pl.BlockSpec(memory_space=pltpu.SMEM),
                    pl.BlockSpec(memory_space=pltpu.SMEM),
                ],
                out_specs=[
                    pl.BlockSpec(memory_space=pl.ANY),
                    pl.BlockSpec(memory_space=pltpu.SMEM),
                    pl.BlockSpec(memory_space=pltpu.SMEM),
                ],
                scratch_shapes=[pltpu.VMEM((rows, cols), jnp.bfloat16)]
                + [pltpu.VMEM((arrivals, part, cols), jnp.bfloat16)] * chunks
                + [pltpu.VMEM((slots, part, width), jnp.float32)] * chunks
                + [
                    pltpu.SMEM((slots,), jnp.int32),
                    pltpu.SMEM((slots,), jnp.float32),
                    pltpu.SMEM((slots,), jnp.int32),
                    pltpu.VMEM((blocks, part, width), jnp.float32),
                    pltpu.VMEM((slots, 8, width), jnp.float32),
                    pltpu.VMEM((1, LANES), jnp.float32),
                    pltpu.VMEM((shards - 1, 1, LANES), jnp.float32),
                    pltpu.VMEM((1, LANES), jnp.float32),
                    pltpu.VMEM((groups - 1, 1, LANES), jnp.float32),
                    dma,
                    dma((chunks, arrivals)),
                    dma((chunks, arrivals)),
                    dma((chunks, shards - 1)),
                    dma((chunks, shards - 1)),
                    dma((chunks,)),
                    dma((shards - 1,)),
                    dma((shards - 1,)),
                    dma((groups - 1,)),
                    dma((groups - 1,)),
                ]
                + [
                    pltpu.VMEM((2, rows, cols), jnp.bfloat16),
                    pltpu.VMEM((chunks, 2, part, cols), jnp.bfloat16),
                    pltpu.VMEM((chunks, 2, blocks // 2, 3, 8, width), jnp.int32),
                    pltpu.VMEM((chunks, 2, 1, LANES), jnp.float32),
                    pltpu.VMEM((chunks, blocks // 2, 3, 8, width), jnp.int32),
                    pltpu.VMEM((chunks, 1, LANES), jnp.float32),
                    pltpu.VMEM((2, part, cols), jnp.bfloat16),
                    dma((2,)),
                    dma((chunks, 2)),
                    dma((chunks, 2)),
                    dma((chunks, 2, 2)),
                    dma((chunks, 2)),
                    dma((2,)),
                    dma((2,)),
                ]
                * relay,
                compiler_params=pltpu.CompilerParams(
                    collective_id=0,
                    has_side_effects=True,
                    vmem_limit_bytes=60 * 1024 * 1024,
                ),
            )(x, joined, slot)
        )

    return jax.shard_map(
        step,
        mesh=mesh,
        in_specs=(P("grp", "shard", None), P(), P()),
        out_specs=(P("shard", None, "grp", None), P("shard"), P()),
        check_vma=False,
    )
```

profile of v0, /device:TPU:0, one launch (start us, length us, event | category | flops | bytes accessed | tf_op | source)
XLA Modules:
  0.0 130.1 jit_solution(8208010686694341529)
XLA Ops:
  0.6 124.5 %shard_map.58 = (f32[6,8,128,128]{3,2,1,0:T(8,128)}, f32[6]{0:T(128)}, f32[3]{0:T(128)}) custom-call(bf16[1,512,6144]{2,1,0:T(8,128)(2,1)} %refs_0_.1, s32[48]{0:T(128)} %refs_1_.1, s32[48]{0:T(128)} %refs_2_.1), custom_call_target="tpu_custom_call" | custom-call | tf_op jit(solution)/shard_map/pallas_call | solution.py:395
  125.1 0.0 copy-start.1
  125.1 0.0 copy-start
  125.1 3.9 %copy.9 = f32[6,8,128,128]{3,2,1,0:T(8,128)} copy(f32[6,8,128,128]{3,2,1,0:T(8,128)} %get-tuple-element.6) | data formatting | bytes 6291456
  129.0 0.0 copy-done.1
  129.1 0.5 copy.10
  129.6 0.0 copy-done
  129.6 0.5 copy.11
Async XLA Ops:
  125.1 3.9 %copy-start.1 = (f32[6]{0:T(128)S(1)}, f32[6]{0:T(128)}, u32[]{:S(2)}) copy-start(f32[6]{0:T(128)} %get-tuple-element.7) | copy-start | bytes 76
  125.1 4.4 %copy-start = (f32[3]{0:T(128)S(1)}, f32[3]{0:T(128)}, u32[]{:S(2)}) copy-start(f32[3]{0:T(128)} %get-tuple-element.8) | copy-start | bytes 40
where the time goes:
time: 130 us
  Pallas kernels  124 us (95%)
  local copies, waits for them, and re-layouts  4.94 us (4%)
    pallas_call x1, Pallas kernels, step(): pl.pallas_call(functools.partial(kernel, groups, shards, blocks, slots_de...  124 us
    unnamed x7, local copies, waits for them, and re-layouts  4.94 us

commit v1 on v0

v1 whole, which is shorter than its diff:
```python
import functools

import jax
import jax.numpy as jnp
from jax import lax
from jax.experimental import pallas as pl
from jax.experimental.pallas import tpu as pltpu
from jax.sharding import PartitionSpec as P

D = 4096
QH = 32
KVH = 8
HS = 128
LANES = 128
MESH = pl.DeviceIdType.MESH


def chunk_rows(rows):
    return 16 if rows % 16 == 0 else rows


PART = 8
GROUP = 8
QMAX = 524286.0
SMALL = 2.0**-64
PLAN = (("RRM", 8), ("M", 8))


def encode(tiles):
    peak = functools.reduce(jnp.maximum, [jnp.abs(t) for t in tiles])
    peak = jnp.max(peak, axis=0, keepdims=True)
    lift = jnp.where(peak < SMALL, 1.0 / SMALL, 1.0)
    scale = QMAX / jnp.maximum(peak * lift, SMALL)
    codes = [jnp.round(t * lift * scale).astype(jnp.int32) for t in tiles]
    half = GROUP // 2
    words = [(codes[i] << 12) | (codes[half + i] & 4095) for i in range(half)]
    tops = [((codes[half + i] >> 12) & 255) << (8 * i) for i in range(half)]
    words.append(functools.reduce(jnp.bitwise_or, tops))
    return words, peak


def decode(words, peak):
    half = GROUP // 2
    codes = [words[i] >> 12 for i in range(half)]
    for i in range(half):
        top = (words[half] << (24 - 8 * i)) >> 24
        codes.append((top << 12) | (words[i] & 4095))
    return [c.astype(jnp.float32) * (1.0 / QMAX) * peak for c in codes]


def flip(s, o):
    for b in range(3):
        if o >> b & 1:
            s = s + (1 - 2 * lax.rem(lax.div(s, 1 << b), 2)) * (1 << b)
    return s


def line_kernel(
    blocks,
    slots_dev,
    x_ref,
    joined_ref,
    slot_ref,
    out_ref,
    head_ref,
    type_ref,
    own,
    far,
    passed,
    got,
    out_words,
    out_peaks,
    in_words,
    in_peaks,
    ready,
    source,
    taken,
    kind_of,
    summed,
    squares,
    grp_part,
    grp_all,
    shard_part,
    shard_all,
    own_sem,
    far_sem,
    plane_sem,
    beyond_sem,
    r_send,
    r_recv,
    m_send,
    m_recv,
    w_send,
    w_recv,
    p_send,
    p_recv,
    a_send,
    a_recv,
    keep_sem,
    g_send,
    g_recv,
    s_send,
    s_recv,
):
    groups, shards = 4, 8
    grp = lax.axis_index("grp")
    shard = lax.axis_index("shard")
    slots = slots_dev * shards
    chunks = own.shape[0]
    width = own.shape[2] // blocks
    sets = blocks // GROUP
    span = GROUP * width

    outer = (grp == 0) | (grp == groups - 1)
    inner = jnp.logical_not(outer)
    mate = grp + 1 - 2 * lax.rem(grp, 2)
    near = jnp.where(outer, 3 - mate, 3 - grp)
    beyond = near + 1 - 2 * lax.rem(near, 2)
    dests = (near, beyond)

    own_copy = pltpu.make_async_copy(x_ref.at[pl.ds(grp * chunks, chunks)], own, own_sem)

    def far_copy(f):
        return pltpu.make_async_copy(
            x_ref.at[pl.ds(dests[f] * chunks, chunks)], far.at[f], far_sem.at[f]
        )

    def send(src, dst, send_sem, recv_sem, to):
        return pltpu.make_async_remote_copy(
            src_ref=src,
            dst_ref=dst,
            send_sem=send_sem,
            recv_sem=recv_sem,
            device_id=to,
            device_id_type=MESH,
        )

    def relay_copy(c, f):
        src = x_ref.at[dests[f] * chunks + c]
        return send(src, passed.at[c, f], r_send.at[c, f], r_recv.at[c, f], (mate, shard))

    def mate_copy(c):
        src = x_ref.at[mate * chunks + c]
        return send(src, got.at[c], m_send.at[c], m_recv.at[c], (mate, shard))

    def coded_copies(c, f):
        to = (dests[f], shard)
        return (
            send(out_words.at[c, f], in_words.at[c], w_send.at[c, f], w_recv.at[c], to),
            send(out_peaks.at[c, f], in_peaks.at[c], p_send.at[c, f], p_recv.at[c], to),
        )

    order = (6, 7, 2, 4, 3, 5, 1)

    def rows_copy(c, o):
        to = flip(shard, o)
        return send(
            ready.at[c, pl.ds(to * slots_dev, slots_dev)],
            out_ref.at[:, shard, pl.ds(pl.multiple_of(c * PART, PART), PART), :],
            a_send.at[c, o - 1],
            a_recv.at[c, o - 1],
            (grp, to),
        )

    def keep_copy(c):
        return pltpu.make_async_copy(
            ready.at[c, pl.ds(shard * slots_dev, slots_dev)],
            out_ref.at[:, shard, pl.ds(pl.multiple_of(c * PART, PART), PART), :],
            keep_sem.at[c],
        )

    def settle(c):
        for o in order:
            rows_copy(c, o).wait()
        keep_copy(c).wait()

    own_copy.start()

    barrier = pltpu.get_barrier_semaphore()
    pl.semaphore_signal(barrier, 1, device_id=(mate, shard), device_id_type=MESH)
    for o in range(1, 6):
        pl.semaphore_signal(barrier, 1, device_id=(grp, flip(shard, o)), device_id_type=MESH)

    @pl.when(inner)
    def _():
        pl.semaphore_signal(barrier, 1, device_id=(near, shard), device_id_type=MESH)
        pl.semaphore_wait(barrier, 7)
        pl.semaphore_signal(beyond_sem, 1, device_id=(near, shard), device_id_type=MESH)
        for f in range(2):
            far_copy(f).start()

    @pl.when(outer)
    def _():
        pl.semaphore_wait(barrier, 6)
        r = m = 0
        for pattern, times in PLAN:
            nr, nm = pattern.count("R"), pattern.count("M")

            def queue(k, carry, pattern=pattern, r=r, m=m, nr=nr, nm=nm):
                i = j = 0
                for kind in pattern:
                    if kind == "R":
                        for f in range(2):
                            relay_copy(r + k * nr + i, f).start()
                        i += 1
                    else:
                        mate_copy(m + k * nm + j).start()
                        j += 1
                return carry

            lax.fori_loop(0, times, queue, 0)
            r, m = r + times * nr, m + times * nm

    pl.semaphore_signal(plane_sem, 1, device_id=(grp, flip(shard, 2)), device_id_type=MESH)

    def find(j, carry):
        head = jnp.int32(-1)
        for b in range(blocks):
            head = jnp.where(slot_ref[b] == j, b, head)
        there = head >= 0
        source[j] = jnp.where(there, joined_ref[jnp.maximum(head, 0)], 0)
        taken[j] = jnp.where(there, 1.0, 0.0)
        kind = jnp.where(head >= QH, 1, 0) + jnp.where(head >= QH + KVH, 1, 0)
        kind_of[j] = jnp.where(there, kind, 3)
        return carry

    lax.fori_loop(0, slots, find, 0)
    own_copy.wait()

    def clear(j, carry):
        squares[j] = jnp.zeros((PART, width), jnp.float32)
        return carry

    lax.fori_loop(0, slots, clear, 0)

    def pack(c):
        mate_copy(c).start()
        for f in range(2):
            relay_copy(c, f).wait_recv()

            def pack_set(p, carry, f=f):
                at = pl.ds(pl.multiple_of(p * span, span), span)
                total = far[f, c, :, at].astype(jnp.float32) + passed[c, f, :, at].astype(jnp.float32)
                words, peak = encode([total[:, i * width : (i + 1) * width] for i in range(GROUP)])
                for i, word in enumerate(words):
                    out_words[c, f, p, i] = word
                out_peaks[c, f, p] = peak
                return carry

            lax.fori_loop(0, sets, pack_set, 0, unroll=2)
            for copy in coded_copies(c, f):
                copy.start()

    def finish(c):
        for copy in coded_copies(c, 0):
            copy.wait_recv()

        def pre_set(p, carry):
            at = pl.ds(pl.multiple_of(p * span, span), span)
            mine = own[c, :, at].astype(jnp.float32)
            tiles = decode([in_words[c, p, i] for i in range(GROUP // 2 + 1)], in_peaks[c, p])
            for i, tile in enumerate(tiles):
                summed[p * GROUP + i] = mine[:, i * width : (i + 1) * width] + tile
            return carry

        lax.fori_loop(0, sets, pre_set, 0, unroll=2)
        mate_copy(c).wait_recv()

        def add_set(p, carry):
            at = pl.ds(pl.multiple_of(p * span, span), span)
            more = got[c, :, at].astype(jnp.float32)
            for i in range(GROUP):
                summed[p * GROUP + i] += more[:, i * width : (i + 1) * width]
            return carry

        lax.fori_loop(0, sets, add_set, 0, unroll=2)

        def place(j, carry):
            total = summed[source[j]] * taken[j]
            ready[c, j] = total
            squares[j] += total * total
            return carry

        lax.fori_loop(0, slots, place, 0, unroll=8)
        for o in order:
            rows_copy(c, o).start()
        keep_copy(c).start()

    LAG = 3

    def finish_and_settle(c, carry=0):
        finish(c)

        @pl.when(c >= LAG)
        def _():
            settle(c - LAG)

        return carry

    @pl.when(inner)
    def _():
        for f in range(2):
            far_copy(f).wait()
        pl.semaphore_wait(beyond_sem, 1)
        pl.semaphore_wait(plane_sem, 1)
        r = m = 0
        for pattern, times in PLAN:
            nr, nm = pattern.count("R"), pattern.count("M")

            def act(k, carry, pattern=pattern, r=r, m=m, nr=nr, nm=nm):
                i = j = 0
                for kind in pattern:
                    if kind == "R":
                        pack(r + k * nr + i)
                        i += 1
                    else:
                        finish_and_settle(m + k * nm + j)
                        j += 1
                return carry

            lax.fori_loop(0, times, act, 0)
            r, m = r + times * nr, m + times * nm

    @pl.when(outer)
    def _():
        pl.semaphore_wait(plane_sem, 1)
        lax.fori_loop(0, chunks, finish_and_settle, 0)

    lane = lax.broadcasted_iota(jnp.int32, (slots, LANES), 1)
    row = lax.broadcasted_iota(jnp.int32, (slots, LANES), 0)
    per_slot = jnp.sum(jnp.sum(squares[...], axis=1), axis=1, keepdims=True)
    total = jnp.sum(jnp.where(lane == row, per_slot, 0.0), axis=0, keepdims=True)

    def grp_copy(o):
        to = lax.rem(grp + o, groups)
        return send(grp_part, grp_all.at[o - 1], g_send.at[o - 1], g_recv.at[o - 1], (to, shard))

    def shard_copy(o):
        to = flip(shard, o)
        return send(
            shard_part, shard_all.at[o - 1], s_send.at[o - 1], s_recv.at[o - 1], (grp, to)
        )

    grp_part[...] = total
    for o in range(1, groups):
        grp_copy(o).start()
    lane = lax.broadcasted_iota(jnp.int32, (1, LANES), 1)

    def lay(j, kinds):
        return jnp.where(lane == j, kind_of[j], kinds)

    kinds = lax.fori_loop(0, slots, lay, jnp.full((1, LANES), 3, jnp.int32))

    @pl.when(inner)
    def _():
        def drain(c, carry):
            mate_copy(c).wait_send()
            for f in range(2):
                for copy in coded_copies(c, f):
                    copy.wait_send()
            return carry

        lax.fori_loop(0, chunks, drain, 0)

    @pl.when(outer)
    def _():
        def drain(c, carry):
            mate_copy(c).wait_send()
            for f in range(2):
                relay_copy(c, f).wait_send()
            return carry

        lax.fori_loop(0, chunks, drain, 0)

    for o in range(1, groups):
        grp_copy(o).wait()
        total = total + grp_all[o - 1]
    shard_part[...] = total
    for o in order:
        shard_copy(o).start()
    for c in range(chunks - LAG, chunks):
        settle(c)
    for o in order:
        shard_copy(o).wait()
        total = total + shard_all[o - 1]
    root = jnp.sqrt(total / (D * HS))
    for i in range(slots_dev):
        head_ref[i] = jnp.sum(jnp.where(lane == shard * slots_dev + i, root, 0.0))
    for t, heads in enumerate((QH, KVH, KVH)):
        one = jnp.sum(jnp.where(kinds == t, total, 0.0), axis=1, keepdims=True)
        type_ref[t] = jnp.sum(jnp.sqrt(one / (heads * D * HS)))


def line_step(x, joined, slot, blocks, slots_dev, shards, rows, width):
    chunks = rows // PART
    cols = blocks * width
    sets = blocks // GROUP
    slots = slots_dev * shards
    half = GROUP // 2
    dma = pltpu.SemaphoreType.DMA
    regular = pltpu.SemaphoreType.REGULAR
    f32, i32, bf16 = jnp.float32, jnp.int32, jnp.bfloat16
    return pl.pallas_call(
        functools.partial(line_kernel, blocks, slots_dev),
        out_shape=[
            pltpu.VMEM((slots_dev, shards, rows, width), f32),
            jax.ShapeDtypeStruct((slots_dev,), f32),
            jax.ShapeDtypeStruct((3,), f32),
        ],
        in_specs=[
            pl.BlockSpec(memory_space=pltpu.HBM),
            pl.BlockSpec(memory_space=pltpu.SMEM),
            pl.BlockSpec(memory_space=pltpu.SMEM),
        ],
        out_specs=[
            pl.BlockSpec(memory_space=pltpu.VMEM),
            pl.BlockSpec(memory_space=pltpu.SMEM),
            pl.BlockSpec(memory_space=pltpu.SMEM),
        ],
        scratch_shapes=[
            pltpu.VMEM((chunks, PART, cols), bf16),
            pltpu.VMEM((2, chunks, PART, cols), bf16),
            pltpu.VMEM((chunks, 2, PART, cols), bf16),
            pltpu.VMEM((chunks, PART, cols), bf16),
            pltpu.VMEM((chunks, 2, sets, half + 1, PART, width), i32),
            pltpu.VMEM((chunks, 2, sets, 1, width), f32),
            pltpu.VMEM((chunks, sets, half + 1, PART, width), i32),
            pltpu.VMEM((chunks, sets, 1, width), f32),
            pltpu.VMEM((chunks, slots, PART, width), f32),
            pltpu.SMEM((slots,), i32),
            pltpu.SMEM((slots,), f32),
            pltpu.SMEM((slots,), i32),
            pltpu.VMEM((blocks, PART, width), f32),
            pltpu.VMEM((slots, PART, width), f32),
            pltpu.VMEM((1, LANES), f32),
            pltpu.VMEM((3, 1, LANES), f32),
            pltpu.VMEM((1, LANES), f32),
            pltpu.VMEM((shards - 1, 1, LANES), f32),
            dma,
            dma((2,)),
            regular,
            regular,
            dma((chunks, 2)),
            dma((chunks, 2)),
            dma((chunks,)),
            dma((chunks,)),
            dma((chunks, 2)),
            dma((chunks,)),
            dma((chunks, 2)),
            dma((chunks,)),
            dma((chunks, shards - 1)),
            dma((chunks, shards - 1)),
            dma((chunks,)),
            dma((3,)),
            dma((3,)),
            dma((shards - 1,)),
            dma((shards - 1,)),
        ],
        compiler_params=pltpu.CompilerParams(
            collective_id=0,
            has_side_effects=True,
            vmem_limit_bytes=57 * 1024 * 1024,
        ),
    )(x.reshape(4 * chunks, PART, cols), joined, slot)


def any_kernel(groups, shards, blocks, slots_dev, chunks, *refs):
    x_ref, joined_ref, slot_ref = refs[:3]
    out_ref, head_ref, type_ref = refs[3:6]
    own = refs[6]
    got = refs[7 : 7 + chunks]
    ready = refs[7 + chunks : 7 + 2 * chunks]
    rest = refs[7 + 2 * chunks :]
    (source, taken, kind_of, summed, squares, shard_part, shard_all, grp_part, grp_all) = rest[:9]
    (own_sem, z_send, z_recv, a_send, a_recv, keep_sem, s_send, s_recv, g_send, g_recv) = rest[9:]

    grp = lax.axis_index("grp")
    shard = lax.axis_index("shard")
    slots = slots_dev * shards
    rows = own.shape[0]
    part = rows // chunks
    width = own.shape[1] // blocks

    def grp_peer(offset):
        return lax.rem(grp + offset, groups)

    def shard_peer(offset):
        return lax.rem(shard + offset, shards)

    load_own = pltpu.make_async_copy(
        x_ref.at[0, pl.ds(pl.multiple_of(grp * rows, 8), rows), :], own, own_sem
    )
    load_own.start()

    barrier = pltpu.get_barrier_semaphore()
    for o in range(1, groups):
        pl.semaphore_signal(barrier, 1, device_id=(grp_peer(o), shard), device_id_type=MESH)
    for o in range(1, shards):
        pl.semaphore_signal(barrier, 1, device_id=(grp, shard_peer(o)), device_id_type=MESH)
    pl.semaphore_wait(barrier, groups + shards - 2)

    z_copies = []
    for c in range(chunks):
        for o in range(1, groups):
            first = pl.multiple_of(grp_peer(o) * rows + c * part, 8)
            copy = pltpu.make_async_remote_copy(
                src_ref=x_ref.at[0, pl.ds(first, part), :],
                dst_ref=got[c].at[o - 1],
                send_sem=z_send.at[c, o - 1],
                recv_sem=z_recv.at[c, o - 1],
                device_id=(grp_peer(o), shard),
                device_id_type=MESH,
            )
            copy.start()
            z_copies.append(copy)

    def find(j, carry):
        found, block, kind = jnp.float32(0), jnp.int32(0), jnp.int32(3)
        for b in range(blocks):
            hit = slot_ref[b] == j
            found = jnp.where(hit, 1.0, found)
            block = jnp.where(hit, joined_ref[b], block)
            kind = jnp.where(hit, (b >= QH) + (b >= QH + KVH), kind)
        source[j] = block
        taken[j] = found
        kind_of[j] = kind
        return carry

    lax.fori_loop(0, slots, find, 0)

    load_own.wait()
    a_copies = []
    for c in range(chunks):
        for o in range(1, groups):
            z_copies[c * (groups - 1) + o - 1].wait_recv()

        def add(k, carry):
            at = pl.multiple_of(k * width, width)
            total = own[c * part : (c + 1) * part, pl.ds(at, width)].astype(jnp.float32)
            for o in range(1, groups):
                total += got[c][o - 1, :, pl.ds(at, width)].astype(jnp.float32)
            summed[k] = total
            return carry

        lax.fori_loop(0, blocks, add, 0, unroll=4)

        def slot(j, carry):
            total = summed[source[j]] * taken[j]
            ready[c][j] = total
            sq = jnp.sum((total * total).reshape(part // 8, 8, width), axis=0)
            squares[j] = sq if c == 0 else squares[j] + sq
            return carry

        lax.fori_loop(0, slots, slot, 0, unroll=4)

        if c == chunks - 1:
            lane = lax.broadcasted_iota(jnp.int32, (slots, LANES), 1)
            row = lax.broadcasted_iota(jnp.int32, (slots, LANES), 0)
            per_slot = jnp.sum(jnp.sum(squares[...], axis=1), axis=1, keepdims=True)
            shard_part[...] = jnp.sum(jnp.where(lane == row, per_slot, 0.0), axis=0, keepdims=True)
            s_copies = []
            for o in range(1, shards):
                copy = pltpu.make_async_remote_copy(
                    src_ref=shard_part,
                    dst_ref=shard_all.at[o - 1],
                    send_sem=s_send.at[o - 1],
                    recv_sem=s_recv.at[o - 1],
                    device_id=(grp, shard_peer(o)),
                    device_id_type=MESH,
                )
                copy.start()
                s_copies.append(copy)

        for o in range(1, shards):
            copy = pltpu.make_async_remote_copy(
                src_ref=ready[c].at[pl.ds(shard_peer(o) * slots_dev, slots_dev)],
                dst_ref=out_ref.at[:, shard, pl.ds(c * part, part), :],
                send_sem=a_send.at[c, o - 1],
                recv_sem=a_recv.at[c, o - 1],
                device_id=(grp, shard_peer(o)),
                device_id_type=MESH,
            )
            copy.start()
            a_copies.append(copy)
        copy = pltpu.make_async_copy(
            ready[c].at[pl.ds(shard * slots_dev, slots_dev)],
            out_ref.at[:, shard, pl.ds(c * part, part), :],
            keep_sem.at[c],
        )
        copy.start()
        a_copies.append(copy)

    total = shard_part[...]
    for o in range(1, shards):
        s_copies[o - 1].wait()
        total = total + shard_all[o - 1]
    grp_part[...] = total
    g_copies = []
    for o in range(1, groups):
        copy = pltpu.make_async_remote_copy(
            src_ref=grp_part,
            dst_ref=grp_all.at[o - 1],
            send_sem=g_send.at[o - 1],
            recv_sem=g_recv.at[o - 1],
            device_id=(grp_peer(o), shard),
            device_id_type=MESH,
        )
        copy.start()
        g_copies.append(copy)
    lane = lax.broadcasted_iota(jnp.int32, (1, LANES), 1)

    def lay(j, kinds):
        return jnp.where(lane == j, kind_of[j], kinds)

    kinds = lax.fori_loop(0, slots, lay, jnp.full((1, LANES), 3, jnp.int32))
    for o in range(1, groups):
        g_copies[o - 1].wait()
        total = total + grp_all[o - 1]
    root = jnp.sqrt(total / (D * HS))
    for i in range(slots_dev):
        head_ref[i] = jnp.sum(jnp.where(lane == shard * slots_dev + i, root, 0.0))
    for t, heads in enumerate((QH, KVH, KVH)):
        one = jnp.sum(jnp.where(kinds == t, total, 0.0), axis=1, keepdims=True)
        type_ref[t] = jnp.sum(jnp.sqrt(one / (heads * D * HS)))

    for copy in z_copies:
        copy.wait_send()
    for copy in a_copies:
        copy.wait()


def any_step(x, joined, slot, groups, shards, blocks, slots_dev, rows, width):
    slots = slots_dev * shards
    cols = blocks * width
    part = chunk_rows(rows)
    chunks = rows // part
    dma = pltpu.SemaphoreType.DMA
    return pl.pallas_call(
        functools.partial(any_kernel, groups, shards, blocks, slots_dev, chunks),
        out_shape=[
            jax.ShapeDtypeStruct((slots_dev, shards, rows, width), jnp.float32),
            jax.ShapeDtypeStruct((slots_dev,), jnp.float32),
            jax.ShapeDtypeStruct((3,), jnp.float32),
        ],
        in_specs=[
            pl.BlockSpec(memory_space=pltpu.HBM),
            pl.BlockSpec(memory_space=pltpu.SMEM),
            pl.BlockSpec(memory_space=pltpu.SMEM),
        ],
        out_specs=[
            pl.BlockSpec(memory_space=pl.ANY),
            pl.BlockSpec(memory_space=pltpu.SMEM),
            pl.BlockSpec(memory_space=pltpu.SMEM),
        ],
        scratch_shapes=[pltpu.VMEM((rows, cols), jnp.bfloat16)]
        + [pltpu.VMEM((groups - 1, part, cols), jnp.bfloat16)] * chunks
        + [pltpu.VMEM((slots, part, width), jnp.float32)] * chunks
        + [
            pltpu.SMEM((slots,), jnp.int32),
            pltpu.SMEM((slots,), jnp.float32),
            pltpu.SMEM((slots,), jnp.int32),
            pltpu.VMEM((blocks, part, width), jnp.float32),
            pltpu.VMEM((slots, 8, width), jnp.float32),
            pltpu.VMEM((1, LANES), jnp.float32),
            pltpu.VMEM((shards - 1, 1, LANES), jnp.float32),
            pltpu.VMEM((1, LANES), jnp.float32),
            pltpu.VMEM((groups - 1, 1, LANES), jnp.float32),
            dma,
            dma((chunks, groups - 1)),
            dma((chunks, groups - 1)),
            dma((chunks, shards - 1)),
            dma((chunks, shards - 1)),
            dma((chunks,)),
            dma((shards - 1,)),
            dma((shards - 1,)),
            dma((groups - 1,)),
            dma((groups - 1,)),
        ],
        compiler_params=pltpu.CompilerParams(
            collective_id=0,
            has_side_effects=True,
            vmem_limit_bytes=60 * 1024 * 1024,
        ),
    )(x, joined, slot)


def solution(mesh):
    groups, shards = mesh.shape["grp"], mesh.shape["shard"]

    def step(x, joined, slot):
        blocks = joined.shape[0]
        slots_dev = (blocks + shards - 1) // shards
        rows = x.shape[1] // groups
        width = x.shape[2] // blocks
        line = groups == 4 and shards == 8 and rows == 16 * PART and blocks % GROUP == 0
        if line and width == LANES and slots_dev * shards <= LANES:
            return tuple(line_step(x, joined, slot, blocks, slots_dev, shards, rows, width))
        return tuple(any_step(x, joined, slot, groups, shards, blocks, slots_dev, rows, width))

    return jax.shard_map(
        step,
        mesh=mesh,
        in_specs=(P("grp", "shard", None), P(), P()),
        out_specs=(P("shard", None, "grp", None), P("shard"), P()),
        check_vma=False,
    )
```

time: 130 us -> 123 us (0.946)
  Pallas kernels: 124 us -> 120 us
  local copies, waits for them, and re-layouts: 4.94 us -> 2.7 us
    pallas_call x1, Pallas kernels: 124 us -> 120 us  [line_step(): pl.pallas_call(functools.partial(line_kernel, blocks, slots_dev), out_sha...]
    unnamed x7, local copies, waits for them, and re-layouts: 4.94 us -> 2.7 us
where the time goes in v1:
time: 123 us
  Pallas kernels  120 us (98%)
  local copies, waits for them, and re-layouts  2.7 us (2%)
    pallas_call x1, Pallas kernels, line_step(): pl.pallas_call(functools.partial(line_kernel, blocks, slots_dev), out_sha...  120 us
    unnamed x7, local copies, waits for them, and re-layouts  2.7 us

profile of v1, /device:TPU:0, one launch (start us, length us, event | category | flops | bytes accessed | tf_op | source)
XLA Modules:
  0.0 123.3 jit_solution(11033919582873971953)
XLA Ops:
  0.6 119.9 %shard_map.58 = (f32[6,8,128,128]{3,2,1,0:T(8,128)S(1)}, f32[6]{0:T(128)}, f32[3]{0:T(128)}) custom-call(bf16[64,8,6144]{2,1,0:T(8,128)(2,1)} %bitcast.1, s32[48]{0:T(128)} %joined_ref.1, s32[48]{0:T(128)} %slot_ref.1), custom_call_target="tpu_custom_call" | custom-call | tf_op jit(solution)/shard_map/pallas_call | solution.py:403
  120.5 0.0 copy-start.1
  120.5 0.0 copy-start
  120.6 1.7 %copy.9 = f32[6,8,128,128]{3,2,1,0:T(8,128)} copy(f32[6,8,128,128]{3,2,1,0:T(8,128)S(1)} %get-tuple-element.3) | data formatting | bytes 6291456
  122.2 0.0 copy-done.1
  122.2 0.5 copy.10
  122.7 0.0 copy-done
  122.7 0.5 copy.11
Async XLA Ops:
  120.5 1.7 %copy-start.1 = (f32[6]{0:T(128)S(1)}, f32[6]{0:T(128)}, u32[]{:S(2)}) copy-start(f32[6]{0:T(128)} %get-tuple-element.10) | copy-start | bytes 76
  120.5 2.2 %copy-start = (f32[3]{0:T(128)S(1)}, f32[3]{0:T(128)}, u32[]{:S(2)}) copy-start(f32[3]{0:T(128)} %get-tuple-element.11) | copy-start | bytes 40

commit v2 on v1

--- a/solution.py
+++ b/solution.py
@@ -23,7 +23,11 @@
 GROUP = 8
 QMAX = 524286.0
 SMALL = 2.0**-64
-PLAN = (("RRM", 8), ("M", 8))
+LATE = 3
+PLAN = (("FNFNLFNLFNFNLFNMA", 1), ("FNFNM", 5), ("M", 7))
+HOLD = 2
+AHEAD = 4
+LAG = 3
 
 
 def encode(tiles):
@@ -73,6 +77,14 @@
     in_words,
     in_peaks,
     ready,
+    late_src,
+    late_mine,
+    late_in,
+    late_raw,
+    late_words,
+    late_peaks,
+    back_words,
+    back_peaks,
     source,
     taken,
     kind_of,
@@ -101,6 +113,14 @@
     g_recv,
     s_send,
     s_recv,
+    late_sem,
+    lx_send,
+    lx_recv,
+    lk_sem,
+    lf_send,
+    lf_recv,
+    la_send,
+    la_recv,
 ):
     groups, shards = 4, 8
     grp = lax.axis_index("grp")
@@ -174,6 +194,33 @@
             rows_copy(c, o).wait()
         keep_copy(c).wait()
 
+    late_copy = pltpu.make_async_copy(x_ref.at[pl.ds(mate * chunks, LATE)], late_src, late_sem)
+
+    def swap_copy(o):
+        to = flip(shard, o)
+        return send(
+            late_mine.at[:, pl.ds(to * slots_dev, slots_dev)],
+            late_in.at[shard],
+            lx_send.at[o - 1],
+            lx_recv.at[o - 1],
+            (grp, to),
+        )
+
+    stay_copy = pltpu.make_async_copy(
+        late_mine.at[:, pl.ds(shard * slots_dev, slots_dev)], late_in.at[shard], lk_sem
+    )
+
+    def forward_copy(n):
+        to = (mate, shard)
+        return send(late_in.at[:, n], late_raw.at[:, n], lf_send.at[n], lf_recv.at[n], to)
+
+    def back_copies():
+        to = (mate, shard)
+        return (
+            send(late_words, back_words, la_send.at[0], la_recv.at[0], to),
+            send(late_peaks, back_peaks, la_send.at[1], la_recv.at[1], to),
+        )
+
     own_copy.start()
 
     barrier = pltpu.get_barrier_semaphore()
@@ -188,28 +235,30 @@
         pl.semaphore_signal(beyond_sem, 1, device_id=(near, shard), device_id_type=MESH)
         for f in range(2):
             far_copy(f).start()
+        for c in range(AHEAD):
+            mate_copy(c).start()
 
     @pl.when(outer)
     def _():
         pl.semaphore_wait(barrier, 6)
-        r = m = 0
+        done = dict(N=0, F=0, M=LATE)
         for pattern, times in PLAN:
-            nr, nm = pattern.count("R"), pattern.count("M")
-
-            def queue(k, carry, pattern=pattern, r=r, m=m, nr=nr, nm=nm):
-                i = j = 0
+            now, per = dict(done), {k: pattern.count(k) for k in done}
+
+            def queue(k, carry, pattern=pattern, now=now, per=per):
+                at = {key: now[key] + k * per[key] for key in now}
                 for kind in pattern:
-                    if kind == "R":
-                        for f in range(2):
-                            relay_copy(r + k * nr + i, f).start()
-                        i += 1
-                    else:
-                        mate_copy(m + k * nm + j).start()
-                        j += 1
+                    if kind in "NF":
+                        relay_copy(at[kind], "NF".index(kind)).start()
+                    elif kind == "M":
+                        mate_copy(at[kind]).start()
+                    if kind in at:
+                        at[kind] += 1
                 return carry
 
             lax.fori_loop(0, times, queue, 0)
-            r, m = r + times * nr, m + times * nm
+            done = {key: now[key] + times * per[key] for key in now}
+        late_copy.start()
 
     pl.semaphore_signal(plane_sem, 1, device_id=(grp, flip(shard, 2)), device_id_type=MESH)
 
@@ -233,25 +282,28 @@
 
     lax.fori_loop(0, slots, clear, 0)
 
-    def pack(c):
-        mate_copy(c).start()
-        for f in range(2):
-            relay_copy(c, f).wait_recv()
-
-            def pack_set(p, carry, f=f):
-                at = pl.ds(pl.multiple_of(p * span, span), span)
-                total = far[f, c, :, at].astype(jnp.float32) + passed[c, f, :, at].astype(jnp.float32)
-                words, peak = encode([total[:, i * width : (i + 1) * width] for i in range(GROUP)])
-                for i, word in enumerate(words):
-                    out_words[c, f, p, i] = word
-                out_peaks[c, f, p] = peak
-                return carry
-
-            lax.fori_loop(0, sets, pack_set, 0, unroll=2)
-            for copy in coded_copies(c, f):
-                copy.start()
-
-    def finish(c):
+    def pack(c, f):
+        relay_copy(c, f).wait_recv()
+
+        def pack_set(p, carry):
+            at = pl.ds(pl.multiple_of(p * span, span), span)
+            total = far[f, c, :, at].astype(jnp.float32) + passed[c, f, :, at].astype(jnp.float32)
+            words, peak = encode([total[:, i * width : (i + 1) * width] for i in range(GROUP)])
+            for i, word in enumerate(words):
+                out_words[c, f, p, i] = word
+            out_peaks[c, f, p] = peak
+            return carry
+
+        lax.fori_loop(0, sets, pack_set, 0, unroll=2)
+        for copy in coded_copies(c, f):
+            copy.start()
+        if f == 1:
+
+            @pl.when(c + AHEAD < chunks)
+            def _():
+                mate_copy(c + AHEAD).start()
+
+    def finish(c, late=False):
         for copy in coded_copies(c, 0):
             copy.wait_recv()
 
@@ -264,7 +316,8 @@
             return carry
 
         lax.fori_loop(0, sets, pre_set, 0, unroll=2)
-        mate_copy(c).wait_recv()
+        if not late:
+            mate_copy(c).wait_recv()
 
         def add_set(p, carry):
             at = pl.ds(pl.multiple_of(p * span, span), span)
@@ -273,12 +326,14 @@
                 summed[p * GROUP + i] += more[:, i * width : (i + 1) * width]
             return carry
 
-        lax.fori_loop(0, sets, add_set, 0, unroll=2)
+        if not late:
+            lax.fori_loop(0, sets, add_set, 0, unroll=2)
 
         def place(j, carry):
             total = summed[source[j]] * taken[j]
             ready[c, j] = total
-            squares[j] += total * total
+            if not late:
+                squares[j] += total * total
             return carry
 
         lax.fori_loop(0, slots, place, 0, unroll=8)
@@ -286,12 +341,19 @@
             rows_copy(c, o).start()
         keep_copy(c).start()
 
-    LAG = 3
-
-    def finish_and_settle(c, carry=0):
+    def tell(j, carry):
+        for n in range(LATE):
+            at = pl.ds(n * PART, PART)
+            words, peak = encode([out_ref[j, a, at, :] for a in range(shards)])
+            for i, word in enumerate(words):
+                late_words[n, j, i] = word
+            late_peaks[n, j] = peak
+        return carry
+
+    def finish_and_settle(c, carry=0, first=0):
         finish(c)
 
-        @pl.when(c >= LAG)
+        @pl.when(c >= first + LAG)
         def _():
             settle(c - LAG)
 
@@ -303,28 +365,77 @@
             far_copy(f).wait()
         pl.semaphore_wait(beyond_sem, 1)
         pl.semaphore_wait(plane_sem, 1)
-        r = m = 0
+        done = dict(N=0, F=0, L=0, M=LATE)
         for pattern, times in PLAN:
-            nr, nm = pattern.count("R"), pattern.count("M")
-
-            def act(k, carry, pattern=pattern, r=r, m=m, nr=nr, nm=nm):
-                i = j = 0
+            now, per = dict(done), {k: pattern.count(k) for k in done}
+
+            def act(k, carry, pattern=pattern, now=now, per=per):
+                at = {key: now[key] + k * per[key] for key in now}
                 for kind in pattern:
-                    if kind == "R":
-                        pack(r + k * nr + i)
-                        i += 1
+                    if kind in "NF":
+                        pack(at[kind], "NF".index(kind))
+                    elif kind == "M":
+                        finish_and_settle(at[kind], first=LATE)
+                    elif kind == "L":
+                        finish(at[kind], late=True)
                     else:
-                        finish_and_settle(m + k * nm + j)
-                        j += 1
+                        for c in range(LATE):
+                            settle(c)
+                        lax.fori_loop(0, slots_dev, tell, 0)
+                        for copy in back_copies():
+                            copy.start()
+                    if kind in at:
+                        at[kind] += 1
                 return carry
 
             lax.fori_loop(0, times, act, 0)
-            r, m = r + times * nr, m + times * nm
+            done = {key: now[key] + times * per[key] for key in now}
 
     @pl.when(outer)
     def _():
         pl.semaphore_wait(plane_sem, 1)
-        lax.fori_loop(0, chunks, finish_and_settle, 0)
+        late_copy.wait()
+
+        for n in range(LATE):
+
+            def split(p, carry, n=n):
+                at = pl.ds(pl.multiple_of(p * span, span), span)
+                rows = late_src[n, :, at].astype(jnp.float32)
+                for i in range(GROUP):
+                    summed[p * GROUP + i] = rows[:, i * width : (i + 1) * width]
+                return carry
+
+            lax.fori_loop(0, sets, split, 0, unroll=2)
+
+            def arrange(j, carry, n=n):
+                late_mine[n, j] = (summed[source[j]] * taken[j]).astype(jnp.bfloat16)
+                return carry
+
+            lax.fori_loop(0, slots, arrange, 0, unroll=4)
+        for o in order:
+            swap_copy(o).start()
+        stay_copy.start()
+        for o in order:
+            swap_copy(o).wait()
+        stay_copy.wait()
+        for n in range(LATE - HOLD):
+            forward_copy(n).start()
+        lax.fori_loop(0, chunks - LAG, finish_and_settle, 0)
+        for copy in back_copies():
+            copy.wait_recv()
+
+        def late_squares(j, carry):
+            acc = jnp.zeros((PART, width), jnp.float32)
+            for n in range(LATE):
+                tiles = decode([back_words[n, j, i] for i in range(GROUP // 2 + 1)], back_peaks[n, j])
+                for a, tile in enumerate(tiles):
+                    total = tile + late_in[a, n, j].astype(jnp.float32)
+                    acc += total * total
+            squares[shard * slots_dev + j] += acc
+            return carry
+
+        lax.fori_loop(0, slots_dev, late_squares, 0)
+        lax.fori_loop(chunks - LAG, chunks, finish_and_settle, 0)
 
     lane = lax.broadcasted_iota(jnp.int32, (slots, LANES), 1)
     row = lax.broadcasted_iota(jnp.int32, (slots, LANES), 0)
@@ -344,6 +455,12 @@
     grp_part[...] = total
     for o in range(1, groups):
         grp_copy(o).start()
+
+    @pl.when(outer)
+    def _():
+        for n in range(LATE - HOLD, LATE):
+            forward_copy(n).start()
+
     lane = lax.broadcasted_iota(jnp.int32, (1, LANES), 1)
 
     def lay(j, kinds):
@@ -361,13 +478,19 @@
             return carry
 
         lax.fori_loop(0, chunks, drain, 0)
+        for copy in back_copies():
+            copy.wait_send()
 
     @pl.when(outer)
     def _():
         def drain(c, carry):
-            mate_copy(c).wait_send()
             for f in range(2):
                 relay_copy(c, f).wait_send()
+
+            @pl.when(c >= LATE)
+            def _():
+                mate_copy(c).wait_send()
+
             return carry
 
         lax.fori_loop(0, chunks, drain, 0)
@@ -389,6 +512,24 @@
     for t, heads in enumerate((QH, KVH, KVH)):
         one = jnp.sum(jnp.where(kinds == t, total, 0.0), axis=1, keepdims=True)
         type_ref[t] = jnp.sum(jnp.sqrt(one / (heads * D * HS)))
+
+    @pl.when(outer)
+    def _():
+        for n in range(LATE):
+            forward_copy(n).wait_send()
+
+    @pl.when(inner)
+    def _():
+        for n in range(LATE):
+            forward_copy(n).wait_recv()
+
+            def add_late(a, carry, n=n):
+                for j in range(slots_dev):
+                    at = pl.ds(n * PART, PART)
+                    out_ref[j, a, at, :] += late_raw[a, n, j].astype(jnp.float32)
+                return carry
+
+            lax.fori_loop(0, shards, add_late, 0, unroll=True)
 
 
 def line_step(x, joined, slot, blocks, slots_dev, shards, rows, width):
@@ -427,6 +568,14 @@
             pltpu.VMEM((chunks, sets, half + 1, PART, width), i32),
             pltpu.VMEM((chunks, sets, 1, width), f32),
             pltpu.VMEM((chunks, slots, PART, width), f32),
+            pltpu.VMEM((LATE, PART, cols), bf16),
+            pltpu.VMEM((LATE, slots, PART, width), bf16),
+            pltpu.VMEM((shards, LATE, slots_dev, PART, width), bf16),
+            pltpu.VMEM((shards, LATE, slots_dev, PART, width), bf16),
+            pltpu.VMEM((LATE, slots_dev, half + 1, PART, width), i32),
+            pltpu.VMEM((LATE, slots_dev, 1, width), f32),
+            pltpu.VMEM((LATE, slots_dev, half + 1, PART, width), i32),
+            pltpu.VMEM((LATE, slots_dev, 1, width), f32),
             pltpu.SMEM((slots,), i32),
             pltpu.SMEM((slots,), f32),
             pltpu.SMEM((slots,), i32),
@@ -455,6 +604,14 @@
             dma((3,)),
             dma((shards - 1,)),
             dma((shards - 1,)),
+            dma,
+            dma((shards - 1,)),
+            dma((shards - 1,)),
+            dma,
+            dma((LATE,)),
+            dma((LATE,)),
+            dma((2,)),
+            dma((2,)),
         ],
         compiler_params=pltpu.CompilerParams(
             collective_id=0,

time: 123 us -> 118 us (0.959)
  Pallas kernels: 120 us -> 114 us
    pallas_call x1, Pallas kernels: 120 us -> 114 us  [line_step(): pl.pallas_call(functools.partial(line_kernel, blocks, slots_dev), out_sha...]
where the time goes in v2:
time: 118 us
  Pallas kernels  114 us (97%)
  local copies, waits for them, and re-layouts  2.7 us (2%)
    pallas_call x1, Pallas kernels, line_step(): pl.pallas_call(functools.partial(line_kernel, blocks, slots_dev), out_sha...  114 us
    unnamed x7, local copies, waits for them, and re-layouts  2.7 us

profile of v2, /device:TPU:0, one launch (start us, length us, event | category | flops | bytes accessed | tf_op | source)
XLA Modules:
  0.0 117.7 jit_solution(1744762716577678118)
XLA Ops:
  0.6 114.4 %shard_map.58 = (f32[6,8,128,128]{3,2,1,0:T(8,128)S(1)}, f32[6]{0:T(128)}, f32[3]{0:T(128)}) custom-call(bf16[64,8,6144]{2,1,0:T(8,128)(2,1)} %bitcast.1, s32[48]{0:T(128)} %joined_ref.1, s32[48]{0:T(128)} %slot_ref.1), custom_call_target="tpu_custom_call" | custom-call | tf_op jit(solution)/shard_map/pallas_call | solution.py:544
  115.0 0.0 copy-start.1
  115.0 0.0 copy-start
  115.0 1.7 %copy.9 = f32[6,8,128,128]{3,2,1,0:T(8,128)} copy(f32[6,8,128,128]{3,2,1,0:T(8,128)S(1)} %get-tuple-element.3) | data formatting | bytes 6291456
  116.7 0.0 copy-done.1
  116.7 0.5 copy.10
  117.2 0.0 copy-done
  117.2 0.5 copy.11
Async XLA Ops:
  115.0 1.7 %copy-start.1 = (f32[6]{0:T(128)S(1)}, f32[6]{0:T(128)}, u32[]{:S(2)}) copy-start(f32[6]{0:T(128)} %get-tuple-element.10) | copy-start | bytes 76
  115.0 2.2 %copy-start = (f32[3]{0:T(128)S(1)}, f32[3]{0:T(128)}, u32[]{:S(2)}) copy-start(f32[3]{0:T(128)} %get-tuple-element.11) | copy-start | bytes 40

commit v3 on v2

--- a/solution.py
+++ b/solution.py
@@ -23,9 +23,9 @@
 GROUP = 8
 QMAX = 524286.0
 SMALL = 2.0**-64
-LATE = 3
-PLAN = (("FNFNLFNLFNFNLFNMA", 1), ("FNFNM", 5), ("M", 7))
-HOLD = 2
+LATE = 5
+PLAN = (("FNFNLFNLFNFNLFNLFNFNLMA", 1), ("FNFNM", 4), ("M", 6))
+HOLD = 4
 AHEAD = 4
 LAG = 3
 
@@ -66,8 +66,8 @@
     joined_ref,
     slot_ref,
     out_ref,
-    head_ref,
-    type_ref,
+    total_ref,
+    kinds_ref,
     own,
     far,
     passed,
@@ -506,12 +506,8 @@
     for o in order:
         shard_copy(o).wait()
         total = total + shard_all[o - 1]
-    root = jnp.sqrt(total / (D * HS))
-    for i in range(slots_dev):
-        head_ref[i] = jnp.sum(jnp.where(lane == shard * slots_dev + i, root, 0.0))
-    for t, heads in enumerate((QH, KVH, KVH)):
-        one = jnp.sum(jnp.where(kinds == t, total, 0.0), axis=1, keepdims=True)
-        type_ref[t] = jnp.sum(jnp.sqrt(one / (heads * D * HS)))
+    total_ref[...] = total
+    kinds_ref[...] = kinds
 
     @pl.when(outer)
     def _():
@@ -530,6 +526,30 @@
                 return carry
 
             lax.fori_loop(0, shards, add_late, 0, unroll=True)
+
+
+def store_kernel(slots_dev, in_ref, total_ref, kinds_ref, out_ref, head_ref, type_ref, heads, types, sems):
+    copies = [
+        pltpu.make_async_copy(in_ref.at[j], out_ref.at[j], sems.at[j]) for j in range(slots_dev)
+    ]
+    copies.append(pltpu.make_async_copy(heads, head_ref, sems.at[slots_dev]))
+    copies.append(pltpu.make_async_copy(types, type_ref, sems.at[slots_dev + 1]))
+    for copy in copies[:slots_dev]:
+        copy.start()
+    shard = lax.axis_index("shard")
+    total = total_ref[...]
+    kinds = kinds_ref[...]
+    lane = lax.broadcasted_iota(jnp.int32, (1, LANES), 1)
+    root = jnp.sqrt(total / (D * HS))
+    for i in range(slots_dev):
+        heads[i] = jnp.sum(jnp.where(lane == shard * slots_dev + i, root, 0.0))
+    for t, count in enumerate((QH, KVH, KVH)):
+        one = jnp.sum(jnp.where(kinds == t, total, 0.0), axis=1, keepdims=True)
+        types[t] = jnp.sum(jnp.sqrt(one / (count * D * HS)))
+    for copy in copies[slots_dev:]:
+        copy.start()
+    for copy in copies:
+        copy.wait()
 
 
 def line_step(x, joined, slot, blocks, slots_dev, shards, rows, width):
@@ -541,23 +561,19 @@
     dma = pltpu.SemaphoreType.DMA
     regular = pltpu.SemaphoreType.REGULAR
     f32, i32, bf16 = jnp.float32, jnp.int32, jnp.bfloat16
-    return pl.pallas_call(
+    out, total, kinds = pl.pallas_call(
         functools.partial(line_kernel, blocks, slots_dev),
         out_shape=[
             pltpu.VMEM((slots_dev, shards, rows, width), f32),
-            jax.ShapeDtypeStruct((slots_dev,), f32),
-            jax.ShapeDtypeStruct((3,), f32),
+            pltpu.VMEM((1, LANES), f32),
+            pltpu.VMEM((1, LANES), i32),
         ],
         in_specs=[
             pl.BlockSpec(memory_space=pltpu.HBM),
             pl.BlockSpec(memory_space=pltpu.SMEM),
             pl.BlockSpec(memory_space=pltpu.SMEM),
         ],
-        out_specs=[
-            pl.BlockSpec(memory_space=pltpu.VMEM),
-            pl.BlockSpec(memory_space=pltpu.SMEM),
-            pl.BlockSpec(memory_space=pltpu.SMEM),
-        ],
+        out_specs=[pl.BlockSpec(memory_space=pltpu.VMEM)] * 3,
         scratch_shapes=[
             pltpu.VMEM((chunks, PART, cols), bf16),
             pltpu.VMEM((2, chunks, PART, cols), bf16),
@@ -619,6 +635,22 @@
             vmem_limit_bytes=57 * 1024 * 1024,
         ),
     )(x.reshape(4 * chunks, PART, cols), joined, slot)
+    return pl.pallas_call(
+        functools.partial(store_kernel, slots_dev),
+        out_shape=[
+            jax.ShapeDtypeStruct((slots_dev, shards, rows, width), f32),
+            jax.ShapeDtypeStruct((slots_dev,), f32),
+            jax.ShapeDtypeStruct((3,), f32),
+        ],
+        in_specs=[pl.BlockSpec(memory_space=pltpu.VMEM)] * 3,
+        out_specs=[pl.BlockSpec(memory_space=pltpu.HBM)] * 3,
+        scratch_shapes=[
+            pltpu.SMEM((slots_dev,), f32),
+            pltpu.SMEM((3,), f32),
+            dma((slots_dev + 2,)),
+        ],
+        compiler_params=pltpu.CompilerParams(vmem_limit_bytes=1024 * 1024),
+    )(out, total, kinds)
 
 
 def any_kernel(groups, shards, blocks, slots_dev, chunks, *refs):

time: 118 us -> 113 us (0.958)
  local copies, waits for them, and re-layouts: 2.7 us -> 0 us
  Pallas kernels: 114 us -> 112 us
    pallas_call x1, Pallas kernels: 114 us -> 110 us  [line_step(): pl.pallas_call(functools.partial(line_kernel, blocks, slots_dev), out_sha...]
    unnamed x7 -> x0, local copies, waits for them, and re-layouts: 2.7 us -> none
    pallas_call x0 -> x1, Pallas kernels: none -> 1.75 us  [line_step(): pl.pallas_call(functools.partial(store_kernel, slots_dev), out_shape=[jax...]
where the time goes in v3:
time: 113 us; the launch traced here: 112 us
  Pallas kernels  112 us (99%)
    pallas_call x1, Pallas kernels, line_step(): pl.pallas_call(functools.partial(line_kernel, blocks, slots_dev), out_sha...  110 us

profile of v3, /device:TPU:0, one launch (start us, length us, event | category | flops | bytes accessed | tf_op | source)
XLA Modules:
  0.0 112.4 jit_solution(2575816891299416846)
XLA Ops:
  0.6 110.0 %shard_map.58 = (f32[6,8,128,128]{3,2,1,0:T(8,128)S(1)}, f32[1,128]{1,0:T(1,128)S(1)}, s32[1,128]{1,0:T(1,128)S(1)}) custom-call(bf16[64,8,6144]{2,1,0:T(8,128)(2,1)} %bitcast.1, s32[48]{0:T(128)} %joined_ref.1, s32[48]{0:T(128)} %slot_ref.1), custom_call_target="tpu_custom_call" | custom-call | tf_op jit(solution)/shard_map/pallas_call | solution.py:564
  110.6 1.7 %shard_map.59 = (f32[6,8,128,128]{3,2,1,0:T(8,128)}, f32[6]{0:T(128)}, f32[3]{0:T(128)}) custom-call(f32[6,8,128,128]{3,2,1,0:T(8,128)S(1)} %get-tuple-element.6.in_ref, f32[1,128]{1,0:T(1,128)S(1)} %get-tuple-element.7.total_ref, s32[1,128]{1,0:T(1,128)S(1)} %get-tuple-element.8.kinds_ref), custom_call_target="tpu_custom_call" | custom-call | tf_op jit(solution)/shard_map/pallas_call | solution.py:638

commit v4 on v3

--- a/solution.py
+++ b/solution.py
@@ -24,10 +24,19 @@
 QMAX = 524286.0
 SMALL = 2.0**-64
 LATE = 5
-PLAN = (("FNFNLFNLFNFNLFNLFNFNLMA", 1), ("FNFNM", 4), ("M", 6))
-HOLD = 4
+LATE_COPIES = ((0, 1), (1, 2), (3, 2))
+SINGLE = 2
+PLAN = (("FNFNLfnLflnfnLMfAnm", 1), ("fnm", 3), ("m", 1))
 AHEAD = 4
-LAG = 3
+
+
+def pieces(first, last):
+    c, found = first, []
+    while c < last:
+        n = 2 if c % 2 == 0 and c + 2 <= last and c >= SINGLE else 1
+        found.append((c, n))
+        c += n
+    return found
 
 
 def encode(tiles):
@@ -52,6 +61,19 @@
     return [c.astype(jnp.float32) * (1.0 / QMAX) * peak for c in codes]
 
 
+def piece(c, n):
+    return c if n == 1 else lax.div(c, 2) + SINGLE // 2
+
+
+def wait_for(ref, sem):
+    pltpu.make_async_copy(ref, ref, sem).wait()
+
+
+def steps(pattern, done):
+    per = {k: sum(1 + c.islower() for c in pattern if c.lower() == k) for k in done}
+    return dict(done), per
+
+
 def flip(s, o):
     for b in range(3):
         if o >> b & 1:
@@ -63,11 +85,15 @@
     blocks,
     slots_dev,
     x_ref,
+    joined_hbm,
+    slot_hbm,
+    out_ref,
+    late_raw,
+    total_ref,
+    kinds_ref,
     joined_ref,
     slot_ref,
-    out_ref,
-    total_ref,
-    kinds_ref,
+    first,
     own,
     far,
     passed,
@@ -80,7 +106,6 @@
     late_src,
     late_mine,
     late_in,
-    late_raw,
     late_words,
     late_peaks,
     back_words,
@@ -94,6 +119,8 @@
     grp_all,
     shard_part,
     shard_all,
+    index_sem,
+    first_sem,
     own_sem,
     far_sem,
     plane_sem,
@@ -108,7 +135,7 @@
     p_recv,
     a_send,
     a_recv,
-    keep_sem,
+    a_late,
     g_send,
     g_recv,
     s_send,
@@ -155,44 +182,48 @@
             device_id_type=MESH,
         )
 
-    def relay_copy(c, f):
-        src = x_ref.at[dests[f] * chunks + c]
-        return send(src, passed.at[c, f], r_send.at[c, f], r_recv.at[c, f], (mate, shard))
-
-    def mate_copy(c):
-        src = x_ref.at[mate * chunks + c]
-        return send(src, got.at[c], m_send.at[c], m_recv.at[c], (mate, shard))
-
-    def coded_copies(c, f):
+    index_copies = [
+        pltpu.make_async_copy(joined_hbm, joined_ref, index_sem.at[0]),
+        pltpu.make_async_copy(slot_hbm, slot_ref, index_sem.at[1]),
+    ]
+    first_copy = pltpu.make_async_copy(x_ref.at[pl.ds(beyond * chunks, 1)], first, first_sem)
+
+    def relay_copy(c, n, f):
+        staged = isinstance(c, int) and c == 0 and f == 1
+        src = first if staged else x_ref.at[pl.ds(dests[f] * chunks + c, n)]
+        dst = passed.at[f, pl.ds(c, n)]
+        return send(src, dst, r_send, r_recv.at[piece(c, n), f], (mate, shard))
+
+    def mate_copy(c, n):
+        src = x_ref.at[pl.ds(mate * chunks + c, n)]
+        return send(src, got.at[pl.ds(c, n)], m_send, m_recv.at[lax.div(c, 2)], (mate, shard))
+
+    def coded_copies(c, n, f):
         to = (dests[f], shard)
+        at = pl.ds(c, n)
         return (
-            send(out_words.at[c, f], in_words.at[c], w_send.at[c, f], w_recv.at[c], to),
-            send(out_peaks.at[c, f], in_peaks.at[c], p_send.at[c, f], p_recv.at[c], to),
+            send(out_words.at[f, at], in_words.at[at], w_send, w_recv.at[piece(c, n)], to),
+            send(out_peaks.at[f, at], in_peaks.at[at], p_send, p_recv.at[piece(c, n)], to),
         )
 
     order = (6, 7, 2, 4, 3, 5, 1)
 
-    def rows_copy(c, o):
+    def rows_of(c, n):
+        return pl.ds(pl.multiple_of(c * PART, PART), n * PART)
+
+    def rows_copy(c, n, o, recv_sem):
         to = flip(shard, o)
         return send(
-            ready.at[c, pl.ds(to * slots_dev, slots_dev)],
-            out_ref.at[:, shard, pl.ds(pl.multiple_of(c * PART, PART), PART), :],
-            a_send.at[c, o - 1],
-            a_recv.at[c, o - 1],
+            ready.at[pl.ds(to * slots_dev, slots_dev), rows_of(c, n)],
+            out_ref.at[:, shard, rows_of(c, n), :],
+            a_send,
+            recv_sem,
             (grp, to),
         )
 
-    def keep_copy(c):
-        return pltpu.make_async_copy(
-            ready.at[c, pl.ds(shard * slots_dev, slots_dev)],
-            out_ref.at[:, shard, pl.ds(pl.multiple_of(c * PART, PART), PART), :],
-            keep_sem.at[c],
-        )
-
-    def settle(c):
-        for o in order:
-            rows_copy(c, o).wait()
-        keep_copy(c).wait()
+    def others(first, last):
+        at = pl.ds(first * PART, (last - first) * PART)
+        return ready.at[pl.ds(0, (shards - 1) * slots_dev), at]
 
     late_copy = pltpu.make_async_copy(x_ref.at[pl.ds(mate * chunks, LATE)], late_src, late_sem)
 
@@ -201,8 +232,8 @@
         return send(
             late_mine.at[:, pl.ds(to * slots_dev, slots_dev)],
             late_in.at[shard],
-            lx_send.at[o - 1],
-            lx_recv.at[o - 1],
+            lx_send,
+            lx_recv,
             (grp, to),
         )
 
@@ -210,9 +241,10 @@
         late_mine.at[:, pl.ds(shard * slots_dev, slots_dev)], late_in.at[shard], lk_sem
     )
 
-    def forward_copy(n):
+    def forward_copy(i):
+        at = pl.ds(*LATE_COPIES[i])
         to = (mate, shard)
-        return send(late_in.at[:, n], late_raw.at[:, n], lf_send.at[n], lf_recv.at[n], to)
+        return send(late_in.at[:, at], late_raw.at[:, at], lf_send, lf_recv, to)
 
     def back_copies():
         to = (mate, shard)
@@ -221,7 +253,7 @@
             send(late_peaks, back_peaks, la_send.at[1], la_recv.at[1], to),
         )
 
-    own_copy.start()
+    first_copy.start()
 
     barrier = pltpu.get_barrier_semaphore()
     pl.semaphore_signal(barrier, 1, device_id=(mate, shard), device_id_type=MESH)
@@ -232,32 +264,39 @@
     def _():
         pl.semaphore_signal(barrier, 1, device_id=(near, shard), device_id_type=MESH)
         pl.semaphore_wait(barrier, 7)
+        own_copy.start()
         pl.semaphore_signal(beyond_sem, 1, device_id=(near, shard), device_id_type=MESH)
         for f in range(2):
             far_copy(f).start()
-        for c in range(AHEAD):
-            mate_copy(c).start()
+        for c in range(0, AHEAD, 2):
+            mate_copy(c, 2).start()
 
     @pl.when(outer)
     def _():
         pl.semaphore_wait(barrier, 6)
-        done = dict(N=0, F=0, M=LATE)
+        first_copy.wait()
+        done = dict(n=0, f=0, m=LATE)
         for pattern, times in PLAN:
-            now, per = dict(done), {k: pattern.count(k) for k in done}
+            now, per = steps(pattern, done)
 
             def queue(k, carry, pattern=pattern, now=now, per=per):
                 at = {key: now[key] + k * per[key] for key in now}
                 for kind in pattern:
-                    if kind in "NF":
-                        relay_copy(at[kind], "NF".index(kind)).start()
-                    elif kind == "M":
-                        mate_copy(at[kind]).start()
-                    if kind in at:
-                        at[kind] += 1
+                    n, key = 1 + kind.islower(), kind.lower()
+                    if key in "nf":
+                        relay_copy(at[key], n, "nf".index(key)).start()
+                    elif key == "m":
+                        mate_copy(at[key], n).start()
+                    if key in at:
+                        at[key] += n
                 return carry
 
-            lax.fori_loop(0, times, queue, 0)
+            if times == 1:
+                queue(0, 0)
+            else:
+                lax.fori_loop(0, times, queue, 0)
             done = {key: now[key] + times * per[key] for key in now}
+        own_copy.start()
         late_copy.start()
 
     pl.semaphore_signal(plane_sem, 1, device_id=(grp, flip(shard, 2)), device_id_type=MESH)
@@ -273,6 +312,10 @@
         kind_of[j] = jnp.where(there, kind, 3)
         return carry
 
+    for copy in index_copies:
+        copy.start()
+    for copy in index_copies:
+        copy.wait()
     lax.fori_loop(0, slots, find, 0)
     own_copy.wait()
 
@@ -282,64 +325,81 @@
 
     lax.fori_loop(0, slots, clear, 0)
 
-    def pack(c, f):
-        relay_copy(c, f).wait_recv()
-
-        def pack_set(p, carry):
+    def pack(c, n, f):
+        relay_copy(c, n, f).wait_recv()
+
+        def pack_set(q, carry):
+            i, p = lax.div(q, sets), lax.rem(q, sets)
             at = pl.ds(pl.multiple_of(p * span, span), span)
-            total = far[f, c, :, at].astype(jnp.float32) + passed[c, f, :, at].astype(jnp.float32)
+            total = far[f, c + i, :, at].astype(jnp.float32)
+            total += passed[f, c + i, :, at].astype(jnp.float32)
             words, peak = encode([total[:, i * width : (i + 1) * width] for i in range(GROUP)])
-            for i, word in enumerate(words):
-                out_words[c, f, p, i] = word
-            out_peaks[c, f, p] = peak
+            for w, word in enumerate(words):
+                out_words[f, c + i, p, w] = word
+            out_peaks[f, c + i, p] = peak
             return carry
 
-        lax.fori_loop(0, sets, pack_set, 0, unroll=2)
-        for copy in coded_copies(c, f):
+        lax.fori_loop(0, n * sets, pack_set, 0, unroll=2)
+        for copy in coded_copies(c, n, f):
             copy.start()
-        if f == 1:
-
-            @pl.when(c + AHEAD < chunks)
+        if f == 1 and n == 2:
+
+            @pl.when(c + AHEAD - SINGLE < chunks)
             def _():
-                mate_copy(c + AHEAD).start()
-
-    def finish(c, late=False):
-        for copy in coded_copies(c, 0):
+                mate_copy(c + AHEAD - SINGLE, 2).start()
+
+    def wait_coded(c, n):
+        for copy in coded_copies(c, n, 0):
             copy.wait_recv()
 
-        def pre_set(p, carry):
-            at = pl.ds(pl.multiple_of(p * span, span), span)
-            mine = own[c, :, at].astype(jnp.float32)
-            tiles = decode([in_words[c, p, i] for i in range(GROUP // 2 + 1)], in_peaks[c, p])
-            for i, tile in enumerate(tiles):
-                summed[p * GROUP + i] = mine[:, i * width : (i + 1) * width] + tile
-            return carry
-
-        lax.fori_loop(0, sets, pre_set, 0, unroll=2)
-        if not late:
-            mate_copy(c).wait_recv()
-
-        def add_set(p, carry):
-            at = pl.ds(pl.multiple_of(p * span, span), span)
-            more = got[c, :, at].astype(jnp.float32)
-            for i in range(GROUP):
-                summed[p * GROUP + i] += more[:, i * width : (i + 1) * width]
-            return carry
-
-        if not late:
-            lax.fori_loop(0, sets, add_set, 0, unroll=2)
-
-        def place(j, carry):
-            total = summed[source[j]] * taken[j]
-            ready[c, j] = total
-            if not late:
-                squares[j] += total * total
-            return carry
-
-        lax.fori_loop(0, slots, place, 0, unroll=8)
+    def finish(c, n, arrive):
+        for i in range(n):
+
+            def pre_set(p, carry, i=i):
+                at = pl.ds(pl.multiple_of(p * span, span), span)
+                mine = own[c + i, :, at].astype(jnp.float32)
+                words = [in_words[c + i, p, w] for w in range(GROUP // 2 + 1)]
+                for t, tile in enumerate(decode(words, in_peaks[c + i, p])):
+                    summed[i, p * GROUP + t] = mine[:, t * width : (t + 1) * width] + tile
+                return carry
+
+            lax.fori_loop(0, sets, pre_set, 0, unroll=2)
+        if arrive is not None:
+            arrive()
+        for i in range(n):
+
+            def add_set(p, carry, i=i):
+                at = pl.ds(pl.multiple_of(p * span, span), span)
+                more = got[c + i, :, at].astype(jnp.float32)
+                for t in range(GROUP):
+                    summed[i, p * GROUP + t] += more[:, t * width : (t + 1) * width]
+                return carry
+
+            if arrive is not None:
+                lax.fori_loop(0, sets, add_set, 0, unroll=2)
+
+            def place(j, carry, i=i):
+                total = summed[i, source[j]] * taken[j]
+                ready[j, rows_of(c + i, 1)] = total
+                if arrive is not None:
+                    squares[j] += total * total
+                return carry
+
+            lax.fori_loop(0, slots, place, 0, unroll=8)
         for o in order:
-            rows_copy(c, o).start()
-        keep_copy(c).start()
+            rows_copy(c, n, o, a_late if arrive is None else a_recv).start()
+        mine = ready[pl.ds(shard * slots_dev, slots_dev), rows_of(c, n)]
+        out_ref[:, shard, rows_of(c, n), :] = mine
+
+    def late_chunk(c, n):
+        if c < SINGLE or c % 2 == 0:
+            wait_coded(c, 1 if c < SINGLE else 2)
+        finish(c, n, None)
+
+    def own_chunk(c, n):
+        if n == 2:
+            wait_coded(c, n)
+        finish(c, n, lambda: mate_copy(c, n).wait_recv())
 
     def tell(j, carry):
         for n in range(LATE):
@@ -350,47 +410,41 @@
             late_peaks[n, j] = peak
         return carry
 
-    def finish_and_settle(c, carry=0, first=0):
-        finish(c)
-
-        @pl.when(c >= first + LAG)
-        def _():
-            settle(c - LAG)
-
-        return carry
-
     @pl.when(inner)
     def _():
+        first_copy.wait()
         for f in range(2):
             far_copy(f).wait()
         pl.semaphore_wait(beyond_sem, 1)
         pl.semaphore_wait(plane_sem, 1)
-        done = dict(N=0, F=0, L=0, M=LATE)
+        done = dict(n=0, f=0, l=0, m=LATE)
         for pattern, times in PLAN:
-            now, per = dict(done), {k: pattern.count(k) for k in done}
+            now, per = steps(pattern, done)
 
             def act(k, carry, pattern=pattern, now=now, per=per):
                 at = {key: now[key] + k * per[key] for key in now}
                 for kind in pattern:
-                    if kind in "NF":
-                        pack(at[kind], "NF".index(kind))
-                    elif kind == "M":
-                        finish_and_settle(at[kind], first=LATE)
-                    elif kind == "L":
-                        finish(at[kind], late=True)
+                    n, key = 1 + kind.islower(), kind.lower()
+                    if key in "nf":
+                        pack(at[key], n, "nf".index(key))
+                    elif key == "m":
+                        own_chunk(at[key], n)
+                    elif key == "l":
+                        late_chunk(at[key], n)
                     else:
-                        for c in range(LATE):
-                            settle(c)
+                        wait_for(others(0, LATE), a_late)
                         lax.fori_loop(0, slots_dev, tell, 0)
                         for copy in back_copies():
                             copy.start()
-                    if kind in at:
-                        at[kind] += 1
+                    if key in at:
+                        at[key] += n
                 return carry
 
-            lax.fori_loop(0, times, act, 0)
+            if times == 1:
+                act(0, 0)
+            else:
+                lax.fori_loop(0, times, act, 0)
             done = {key: now[key] + times * per[key] for key in now}
-
     @pl.when(outer)
     def _():
         pl.semaphore_wait(plane_sem, 1)
@@ -402,25 +456,36 @@
                 at = pl.ds(pl.multiple_of(p * span, span), span)
                 rows = late_src[n, :, at].astype(jnp.float32)
                 for i in range(GROUP):
-                    summed[p * GROUP + i] = rows[:, i * width : (i + 1) * width]
+                    summed[0, p * GROUP + i] = rows[:, i * width : (i + 1) * width]
                 return carry
 
             lax.fori_loop(0, sets, split, 0, unroll=2)
 
             def arrange(j, carry, n=n):
-                late_mine[n, j] = (summed[source[j]] * taken[j]).astype(jnp.bfloat16)
+                late_mine[n, j] = (summed[0, source[j]] * taken[j]).astype(jnp.bfloat16)
                 return carry
 
             lax.fori_loop(0, slots, arrange, 0, unroll=4)
         for o in order:
             swap_copy(o).start()
         stay_copy.start()
-        for o in order:
-            swap_copy(o).wait()
         stay_copy.wait()
-        for n in range(LATE - HOLD):
-            forward_copy(n).start()
-        lax.fori_loop(0, chunks - LAG, finish_and_settle, 0)
+        wait_for(late_in.at[pl.ds(0, shards - 1)], lx_recv)
+        forward_copy(0).start()
+
+        def own_pair(k, carry):
+            c = 2 * k
+            finish(c, 2, lambda: mate_copy(c, 2).wait_recv())
+            return carry
+
+        def coded_pair(k, carry):
+            wait_coded(2 * k, 2)
+            return own_pair(k, carry)
+
+        for c, n in pieces(0, 2):
+            wait_coded(c, n)
+        own_pair(0, 0)
+        lax.fori_loop(1, chunks // 2 - 2, coded_pair, 0)
         for copy in back_copies():
             copy.wait_recv()
 
@@ -435,7 +500,7 @@
             return carry
 
         lax.fori_loop(0, slots_dev, late_squares, 0)
-        lax.fori_loop(chunks - LAG, chunks, finish_and_settle, 0)
+        lax.fori_loop(chunks // 2 - 2, chunks // 2, coded_pair, 0)
 
     lane = lax.broadcasted_iota(jnp.int32, (slots, LANES), 1)
     row = lax.broadcasted_iota(jnp.int32, (slots, LANES), 0)
@@ -444,12 +509,12 @@
 
     def grp_copy(o):
         to = lax.rem(grp + o, groups)
-        return send(grp_part, grp_all.at[o - 1], g_send.at[o - 1], g_recv.at[o - 1], (to, shard))
+        return send(grp_part, grp_all.at[o - 1], g_send, g_recv, (to, shard))
 
     def shard_copy(o):
         to = flip(shard, o)
         return send(
-            shard_part, shard_all.at[o - 1], s_send.at[o - 1], s_recv.at[o - 1], (grp, to)
+            shard_part, shard_all.at[o - 1], s_send, s_recv, (grp, to)
         )
 
     grp_part[...] = total
@@ -458,8 +523,8 @@
 
     @pl.when(outer)
     def _():
-        for n in range(LATE - HOLD, LATE):
-            forward_copy(n).start()
+        for i in range(1, len(LATE_COPIES)):
+            forward_copy(i).start()
 
     lane = lax.broadcasted_iota(jnp.int32, (1, LANES), 1)
 
@@ -468,75 +533,91 @@
 
     kinds = lax.fori_loop(0, slots, lay, jnp.full((1, LANES), 3, jnp.int32))
 
-    @pl.when(inner)
-    def _():
-        def drain(c, carry):
-            mate_copy(c).wait_send()
-            for f in range(2):
-                for copy in coded_copies(c, f):
-                    copy.wait_send()
-            return carry
-
-        lax.fori_loop(0, chunks, drain, 0)
-        for copy in back_copies():
-            copy.wait_send()
-
-    @pl.when(outer)
-    def _():
-        def drain(c, carry):
-            for f in range(2):
-                relay_copy(c, f).wait_send()
-
-            @pl.when(c >= LATE)
-            def _():
-                mate_copy(c).wait_send()
-
-            return carry
-
-        lax.fori_loop(0, chunks, drain, 0)
-
+    wait_for(grp_all, g_recv)
     for o in range(1, groups):
-        grp_copy(o).wait()
         total = total + grp_all[o - 1]
     shard_part[...] = total
     for o in order:
         shard_copy(o).start()
-    for c in range(chunks - LAG, chunks):
-        settle(c)
+
+    @pl.when(inner)
+    def _():
+        wait_for(out_words, w_send)
+        wait_for(out_peaks, p_send)
+        wait_for(got, m_send)
+        for copy in back_copies():
+            copy.wait_send()
+        wait_for(others(LATE, chunks), a_recv)
+
+    @pl.when(outer)
+    def _():
+        wait_for(passed, r_send)
+        wait_for(got.at[pl.ds(LATE, chunks - LATE)], m_send)
+        wait_for(late_in.at[pl.ds(0, shards - 1)], lx_send)
+        wait_for(others(0, chunks), a_recv)
+
+    wait_for(others(0, chunks), a_send)
+    wait_for(grp_all, g_send)
+    wait_for(shard_all, s_recv)
+    wait_for(shard_all, s_send)
     for o in order:
-        shard_copy(o).wait()
         total = total + shard_all[o - 1]
     total_ref[...] = total
     kinds_ref[...] = kinds
 
     @pl.when(outer)
     def _():
-        for n in range(LATE):
-            forward_copy(n).wait_send()
+        wait_for(late_in, lf_send)
 
     @pl.when(inner)
     def _():
-        for n in range(LATE):
-            forward_copy(n).wait_recv()
-
-            def add_late(a, carry, n=n):
-                for j in range(slots_dev):
-                    at = pl.ds(n * PART, PART)
-                    out_ref[j, a, at, :] += late_raw[a, n, j].astype(jnp.float32)
-                return carry
-
-            lax.fori_loop(0, shards, add_late, 0, unroll=True)
-
-
-def store_kernel(slots_dev, in_ref, total_ref, kinds_ref, out_ref, head_ref, type_ref, heads, types, sems):
-    copies = [
-        pltpu.make_async_copy(in_ref.at[j], out_ref.at[j], sems.at[j]) for j in range(slots_dev)
+        wait_for(late_raw, lf_recv)
+
+
+def store_kernel(
+    slots_dev,
+    in_ref,
+    late_ref,
+    total_ref,
+    kinds_ref,
+    out_ref,
+    head_ref,
+    type_ref,
+    late_out,
+    heads,
+    types,
+    sems,
+):
+    shards = in_ref.shape[1]
+    late = pl.ds(0, LATE * PART)
+    rest = pl.ds(LATE * PART, in_ref.shape[2] - LATE * PART)
+    bulk = [
+        pltpu.make_async_copy(in_ref.at[j, :, rest], out_ref.at[j, :, rest], sems.at[0, j])
+        for j in range(slots_dev)
     ]
-    copies.append(pltpu.make_async_copy(heads, head_ref, sems.at[slots_dev]))
-    copies.append(pltpu.make_async_copy(types, type_ref, sems.at[slots_dev + 1]))
-    for copy in copies[:slots_dev]:
+    tops = [
+        pltpu.make_async_copy(late_out.at[j], out_ref.at[j, :, late], sems.at[1, j])
+        for j in range(slots_dev)
+    ]
+    small = [
+        pltpu.make_async_copy(heads, head_ref, sems.at[2, 0]),
+        pltpu.make_async_copy(types, type_ref, sems.at[2, 1]),
+    ]
+    for copy in bulk:
         copy.start()
-    shard = lax.axis_index("shard")
+    grp, shard = lax.axis_index("grp"), lax.axis_index("shard")
+    inner = (grp > 0) & (grp < lax.axis_size("grp") - 1)
+    for j in range(slots_dev):
+
+        def add_late(a, carry, j=j):
+            for c in range(LATE):
+                at = pl.ds(c * PART, PART)
+                more = jnp.where(inner, late_ref[a, c, j].astype(jnp.float32), 0.0)
+                late_out[j, a, at, :] = in_ref[j, a, at, :] + more
+            return carry
+
+        lax.fori_loop(0, shards, add_late, 0, unroll=True)
+        tops[j].start()
     total = total_ref[...]
     kinds = kinds_ref[...]
     lane = lax.broadcasted_iota(jnp.int32, (1, LANES), 1)
@@ -546,9 +627,9 @@
     for t, count in enumerate((QH, KVH, KVH)):
         one = jnp.sum(jnp.where(kinds == t, total, 0.0), axis=1, keepdims=True)
         types[t] = jnp.sum(jnp.sqrt(one / (count * D * HS)))
-    for copy in copies[slots_dev:]:
+    for copy in small:
         copy.start()
-    for copy in copies:
+    for copy in bulk + tops + small:
         copy.wait()
 
 
@@ -561,32 +642,31 @@
     dma = pltpu.SemaphoreType.DMA
     regular = pltpu.SemaphoreType.REGULAR
     f32, i32, bf16 = jnp.float32, jnp.int32, jnp.bfloat16
-    out, total, kinds = pl.pallas_call(
+    out, late, total, kinds = pl.pallas_call(
         functools.partial(line_kernel, blocks, slots_dev),
         out_shape=[
             pltpu.VMEM((slots_dev, shards, rows, width), f32),
+            pltpu.VMEM((shards, LATE, slots_dev, PART, width), bf16),
             pltpu.VMEM((1, LANES), f32),
             pltpu.VMEM((1, LANES), i32),
         ],
-        in_specs=[
-            pl.BlockSpec(memory_space=pltpu.HBM),
-            pl.BlockSpec(memory_space=pltpu.SMEM),
-            pl.BlockSpec(memory_space=pltpu.SMEM),
-        ],
-        out_specs=[pl.BlockSpec(memory_space=pltpu.VMEM)] * 3,
+        in_specs=[pl.BlockSpec(memory_space=pltpu.HBM)] * 3,
+        out_specs=[pl.BlockSpec(memory_space=pltpu.VMEM)] * 4,
         scratch_shapes=[
+            pltpu.SMEM((blocks,), i32),
+            pltpu.SMEM((blocks,), i32),
+            pltpu.VMEM((1, PART, cols), bf16),
             pltpu.VMEM((chunks, PART, cols), bf16),
             pltpu.VMEM((2, chunks, PART, cols), bf16),
-            pltpu.VMEM((chunks, 2, PART, cols), bf16),
+            pltpu.VMEM((2, chunks, PART, cols), bf16),
             pltpu.VMEM((chunks, PART, cols), bf16),
-            pltpu.VMEM((chunks, 2, sets, half + 1, PART, width), i32),
-            pltpu.VMEM((chunks, 2, sets, 1, width), f32),
+            pltpu.VMEM((2, chunks, sets, half + 1, PART, width), i32),
+            pltpu.VMEM((2, chunks, sets, 1, width), f32),
             pltpu.VMEM((chunks, sets, half + 1, PART, width), i32),
             pltpu.VMEM((chunks, sets, 1, width), f32),
-            pltpu.VMEM((chunks, slots, PART, width), f32),
+            pltpu.VMEM((slots, rows, width), f32),
             pltpu.VMEM((LATE, PART, cols), bf16),
             pltpu.VMEM((LATE, slots, PART, width), bf16),
-            pltpu.VMEM((shards, LATE, slots_dev, PART, width), bf16),
             pltpu.VMEM((shards, LATE, slots_dev, PART, width), bf16),
             pltpu.VMEM((LATE, slots_dev, half + 1, PART, width), i32),
             pltpu.VMEM((LATE, slots_dev, 1, width), f32),
@@ -595,37 +675,39 @@
             pltpu.SMEM((slots,), i32),
             pltpu.SMEM((slots,), f32),
             pltpu.SMEM((slots,), i32),
-            pltpu.VMEM((blocks, PART, width), f32),
+            pltpu.VMEM((2, blocks, PART, width), f32),
             pltpu.VMEM((slots, PART, width), f32),
             pltpu.VMEM((1, LANES), f32),
             pltpu.VMEM((3, 1, LANES), f32),
             pltpu.VMEM((1, LANES), f32),
             pltpu.VMEM((shards - 1, 1, LANES), f32),
+            dma((2,)),
+            dma,
             dma,
             dma((2,)),
             regular,
             regular,
-            dma((chunks, 2)),
-            dma((chunks, 2)),
-            dma((chunks,)),
-            dma((chunks,)),
-            dma((chunks, 2)),
-            dma((chunks,)),
-            dma((chunks, 2)),
-            dma((chunks,)),
-            dma((chunks, shards - 1)),
-            dma((chunks, shards - 1)),
-            dma((chunks,)),
-            dma((3,)),
-            dma((3,)),
-            dma((shards - 1,)),
-            dma((shards - 1,)),
-            dma,
-            dma((shards - 1,)),
-            dma((shards - 1,)),
-            dma,
-            dma((LATE,)),
-            dma((LATE,)),
+            dma,
+            dma((len(pieces(0, chunks)), 2)),
+            dma,
+            dma((chunks // 2,)),
+            dma,
+            dma((len(pieces(0, chunks)),)),
+            dma,
+            dma((len(pieces(0, chunks)),)),
+            dma,
+            dma,
+            dma,
+            dma,
+            dma,
+            dma,
+            dma,
+            dma,
+            dma,
+            dma,
+            dma,
+            dma,
+            dma,
             dma((2,)),
             dma((2,)),
         ],
@@ -642,15 +724,16 @@
             jax.ShapeDtypeStruct((slots_dev,), f32),
             jax.ShapeDtypeStruct((3,), f32),
         ],
-        in_specs=[pl.BlockSpec(memory_space=pltpu.VMEM)] * 3,
+        in_specs=[pl.BlockSpec(memory_space=pltpu.VMEM)] * 4,
         out_specs=[pl.BlockSpec(memory_space=pltpu.HBM)] * 3,
         scratch_shapes=[
+            pltpu.VMEM((slots_dev, shards, LATE * PART, width), f32),
             pltpu.SMEM((slots_dev,), f32),
             pltpu.SMEM((3,), f32),
-            dma((slots_dev + 2,)),
+            dma((3, slots_dev)),
         ],
-        compiler_params=pltpu.CompilerParams(vmem_limit_bytes=1024 * 1024),
-    )(out, total, kinds)
+        compiler_params=pltpu.CompilerParams(vmem_limit_bytes=4 * 1024 * 1024),
+    )(out, late, total, kinds)
 
 
 def any_kernel(groups, shards, blocks, slots_dev, chunks, *refs):

time: 113 us -> 109 us (0.965)
  Pallas kernels: 112 us -> 108 us
    pallas_call x1, Pallas kernels: 110 us -> 106 us  [line_step(): pl.pallas_call(functools.partial(line_kernel, blocks, slots_dev), out_sha...]
where the time goes in v4:
time: 109 us
  Pallas kernels  108 us (99%)
    pallas_call x1, Pallas kernels, line_step(): pl.pallas_call(functools.partial(line_kernel, blocks, slots_dev), out_sha...  106 us

profile of v4, /device:TPU:0, one launch (start us, length us, event | category | flops | bytes accessed | tf_op | source)
XLA Modules:
  0.0 108.9 jit_solution(1286288547051659362)
XLA Ops:
  0.6 106.4 %shard_map.58 = (f32[6,8,128,128]{3,2,1,0:T(8,128)S(1)}, bf16[8,5,6,8,128]{4,3,2,1,0:T(8,128)(2,1)S(1)}, f32[1,128]{1,0:T(1,128)S(1)}, s32[1,128]{1,0:T(1,128)S(1)}) custom-call(bf16[64,8,6144]{2,1,0:T(8,128)(2,1)} %bitcast.1, s32[48]{0:T(128)} %joined_hbm.1, s32[48]{0:T(128)} %slot_hbm.1), custom_call_target="tpu_custom_call" | custom-call | tf_op jit(solution)/shard_map/pallas_call | solution.py:645
  107.1 1.8 %shard_map.59 = (f32[6,8,128,128]{3,2,1,0:T(8,128)}, f32[6]{0:T(128)}, f32[3]{0:T(128)}) custom-call(f32[6,8,128,128]{3,2,1,0:T(8,128)S(1)} %get-tuple-element.7.in_ref, bf16[8,5,6,8,128]{4,3,2,1,0:T(8,128)(2,1)S(1)} %get-tuple-element.8.late_ref, f32[1,128]{1,0:T(1,128)S(1)} %get-tuple-element.9.total_ref, s32[1,128]{1,0:T(1,128)S(1)} %get-tuple-element.10.kinds_ref), custom_call_target="tpu_custom_call" | custom-call | tf_op jit(solution)/shard_map/pallas_call | solution.py:720

commit v5 on v4

--- a/solution.py
+++ b/solution.py
@@ -21,8 +21,9 @@
 
 PART = 8
 GROUP = 8
-QMAX = 524286.0
-SMALL = 2.0**-64
+BITS = 19
+QMAX = (1 - 2.0**-10) * 2.0 ** (BITS - 2)
+SMALL = 2.0**-120
 LATE = 5
 LATE_COPIES = ((0, 1), (1, 2), (3, 2))
 SINGLE = 2
@@ -39,26 +40,36 @@
     return found
 
 
+def powers(e):
+    half = e >> 1
+    return jnp.exp2(half.astype(jnp.float32)), jnp.exp2((e - half).astype(jnp.float32))
+
+
 def encode(tiles):
     peak = functools.reduce(jnp.maximum, [jnp.abs(t) for t in tiles])
-    peak = jnp.max(peak, axis=0, keepdims=True)
-    lift = jnp.where(peak < SMALL, 1.0 / SMALL, 1.0)
-    scale = QMAX / jnp.maximum(peak * lift, SMALL)
-    codes = [jnp.round(t * lift * scale).astype(jnp.int32) for t in tiles]
-    half = GROUP // 2
-    words = [(codes[i] << 12) | (codes[half + i] & 4095) for i in range(half)]
-    tops = [((codes[half + i] >> 12) & 255) << (8 * i) for i in range(half)]
-    words.append(functools.reduce(jnp.bitwise_or, tops))
-    return words, peak
-
-
-def decode(words, peak):
-    half = GROUP // 2
-    codes = [words[i] >> 12 for i in range(half)]
+    e = jnp.ceil(jnp.log2(jnp.maximum(peak, SMALL))).astype(jnp.int32) - 1
+    p, q = powers(-e)
+    p = p * QMAX
+    codes = [jnp.round(t * q * p).astype(jnp.int32) for t in tiles]
+    half, low = GROUP // 2, 32 - BITS
+    high = BITS - low
+    words = [(codes[i] << low) | (codes[half + i] & ((1 << low) - 1)) for i in range(half)]
+    last = e << 24
     for i in range(half):
-        top = (words[half] << (24 - 8 * i)) >> 24
-        codes.append((top << 12) | (words[i] & 4095))
-    return [c.astype(jnp.float32) * (1.0 / QMAX) * peak for c in codes]
+        last |= ((codes[half + i] >> low) & ((1 << high) - 1)) << (high * i)
+    return words + [last]
+
+
+def decode(words):
+    half, low = GROUP // 2, 32 - BITS
+    high = BITS - low
+    p, q = powers(words[half] >> 24)
+    p = p * (1.0 / QMAX)
+    codes = [words[i] >> low for i in range(half)]
+    for i in range(half):
+        top = (words[half] << (32 - high * (i + 1))) >> (32 - high)
+        codes.append((top << low) | (words[i] & ((1 << low) - 1)))
+    return [c.astype(jnp.float32) * p * q for c in codes]
 
 
 def piece(c, n):
@@ -99,17 +110,13 @@
     passed,
     got,
     out_words,
-    out_peaks,
     in_words,
-    in_peaks,
     ready,
     late_src,
     late_mine,
     late_in,
     late_words,
-    late_peaks,
     back_words,
-    back_peaks,
     source,
     taken,
     kind_of,
@@ -131,8 +138,6 @@
     m_recv,
     w_send,
     w_recv,
-    p_send,
-    p_recv,
     a_send,
     a_recv,
     a_late,
@@ -198,13 +203,10 @@
         src = x_ref.at[pl.ds(mate * chunks + c, n)]
         return send(src, got.at[pl.ds(c, n)], m_send, m_recv.at[lax.div(c, 2)], (mate, shard))
 
-    def coded_copies(c, n, f):
+    def coded_copy(c, n, f):
+        at = pl.ds(c, n)
         to = (dests[f], shard)
-        at = pl.ds(c, n)
-        return (
-            send(out_words.at[f, at], in_words.at[at], w_send, w_recv.at[piece(c, n)], to),
-            send(out_peaks.at[f, at], in_peaks.at[at], p_send, p_recv.at[piece(c, n)], to),
-        )
+        return send(out_words.at[f, at], in_words.at[at], w_send, w_recv.at[piece(c, n)], to)
 
     order = (6, 7, 2, 4, 3, 5, 1)
 
@@ -246,12 +248,7 @@
         to = (mate, shard)
         return send(late_in.at[:, at], late_raw.at[:, at], lf_send, lf_recv, to)
 
-    def back_copies():
-        to = (mate, shard)
-        return (
-            send(late_words, back_words, la_send.at[0], la_recv.at[0], to),
-            send(late_peaks, back_peaks, la_send.at[1], la_recv.at[1], to),
-        )
+    back_copy = send(late_words, back_words, la_send, la_recv, (mate, shard))
 
     first_copy.start()
 
@@ -333,15 +330,13 @@
             at = pl.ds(pl.multiple_of(p * span, span), span)
             total = far[f, c + i, :, at].astype(jnp.float32)
             total += passed[f, c + i, :, at].astype(jnp.float32)
-            words, peak = encode([total[:, i * width : (i + 1) * width] for i in range(GROUP)])
+            words = encode([total[:, i * width : (i + 1) * width] for i in range(GROUP)])
             for w, word in enumerate(words):
                 out_words[f, c + i, p, w] = word
-            out_peaks[f, c + i, p] = peak
             return carry
 
         lax.fori_loop(0, n * sets, pack_set, 0, unroll=2)
-        for copy in coded_copies(c, n, f):
-            copy.start()
+        coded_copy(c, n, f).start()
         if f == 1 and n == 2:
 
             @pl.when(c + AHEAD - SINGLE < chunks)
@@ -349,8 +344,7 @@
                 mate_copy(c + AHEAD - SINGLE, 2).start()
 
     def wait_coded(c, n):
-        for copy in coded_copies(c, n, 0):
-            copy.wait_recv()
+        coded_copy(c, n, 0).wait_recv()
 
     def finish(c, n, arrive):
         for i in range(n):
@@ -359,7 +353,7 @@
                 at = pl.ds(pl.multiple_of(p * span, span), span)
                 mine = own[c + i, :, at].astype(jnp.float32)
                 words = [in_words[c + i, p, w] for w in range(GROUP // 2 + 1)]
-                for t, tile in enumerate(decode(words, in_peaks[c + i, p])):
+                for t, tile in enumerate(decode(words)):
                     summed[i, p * GROUP + t] = mine[:, t * width : (t + 1) * width] + tile
                 return carry
 
@@ -404,10 +398,9 @@
     def tell(j, carry):
         for n in range(LATE):
             at = pl.ds(n * PART, PART)
-            words, peak = encode([out_ref[j, a, at, :] for a in range(shards)])
+            words = encode([out_ref[j, a, at, :] for a in range(shards)])
             for i, word in enumerate(words):
                 late_words[n, j, i] = word
-            late_peaks[n, j] = peak
         return carry
 
     @pl.when(inner)
@@ -434,8 +427,7 @@
                     else:
                         wait_for(others(0, LATE), a_late)
                         lax.fori_loop(0, slots_dev, tell, 0)
-                        for copy in back_copies():
-                            copy.start()
+                        back_copy.start()
                     if key in at:
                         at[key] += n
                 return carry
@@ -486,13 +478,12 @@
             wait_coded(c, n)
         own_pair(0, 0)
         lax.fori_loop(1, chunks // 2 - 2, coded_pair, 0)
-        for copy in back_copies():
-            copy.wait_recv()
+        back_copy.wait_recv()
 
         def late_squares(j, carry):
             acc = jnp.zeros((PART, width), jnp.float32)
             for n in range(LATE):
-                tiles = decode([back_words[n, j, i] for i in range(GROUP // 2 + 1)], back_peaks[n, j])
+                tiles = decode([back_words[n, j, i] for i in range(GROUP // 2 + 1)])
                 for a, tile in enumerate(tiles):
                     total = tile + late_in[a, n, j].astype(jnp.float32)
                     acc += total * total
@@ -543,10 +534,8 @@
     @pl.when(inner)
     def _():
         wait_for(out_words, w_send)
-        wait_for(out_peaks, p_send)
         wait_for(got, m_send)
-        for copy in back_copies():
-            copy.wait_send()
+        back_copy.wait_send()
         wait_for(others(LATE, chunks), a_recv)
 
     @pl.when(outer)
@@ -592,16 +581,16 @@
     late = pl.ds(0, LATE * PART)
     rest = pl.ds(LATE * PART, in_ref.shape[2] - LATE * PART)
     bulk = [
-        pltpu.make_async_copy(in_ref.at[j, :, rest], out_ref.at[j, :, rest], sems.at[0, j])
+        pltpu.make_async_copy(in_ref.at[j, :, rest], out_ref.at[j, :, rest], sems.at[0])
         for j in range(slots_dev)
     ]
     tops = [
-        pltpu.make_async_copy(late_out.at[j], out_ref.at[j, :, late], sems.at[1, j])
+        pltpu.make_async_copy(late_out.at[j], out_ref.at[j, :, late], sems.at[0])
         for j in range(slots_dev)
     ]
     small = [
-        pltpu.make_async_copy(heads, head_ref, sems.at[2, 0]),
-        pltpu.make_async_copy(types, type_ref, sems.at[2, 1]),
+        pltpu.make_async_copy(heads, head_ref, sems.at[1]),
+        pltpu.make_async_copy(types, type_ref, sems.at[2]),
     ]
     for copy in bulk:
         copy.start()
@@ -629,8 +618,9 @@
         types[t] = jnp.sum(jnp.sqrt(one / (count * D * HS)))
     for copy in small:
         copy.start()
-    for copy in bulk + tops + small:
+    for copy in small:
         copy.wait()
+    wait_for(out_ref, sems.at[0])
 
 
 def line_step(x, joined, slot, blocks, slots_dev, shards, rows, width):
@@ -661,17 +651,13 @@
             pltpu.VMEM((2, chunks, PART, cols), bf16),
             pltpu.VMEM((chunks, PART, cols), bf16),
             pltpu.VMEM((2, chunks, sets, half + 1, PART, width), i32),
-            pltpu.VMEM((2, chunks, sets, 1, width), f32),
             pltpu.VMEM((chunks, sets, half + 1, PART, width), i32),
-            pltpu.VMEM((chunks, sets, 1, width), f32),
             pltpu.VMEM((slots, rows, width), f32),
             pltpu.VMEM((LATE, PART, cols), bf16),
             pltpu.VMEM((LATE, slots, PART, width), bf16),
             pltpu.VMEM((shards, LATE, slots_dev, PART, width), bf16),
             pltpu.VMEM((LATE, slots_dev, half + 1, PART, width), i32),
-            pltpu.VMEM((LATE, slots_dev, 1, width), f32),
             pltpu.VMEM((LATE, slots_dev, half + 1, PART, width), i32),
-            pltpu.VMEM((LATE, slots_dev, 1, width), f32),
             pltpu.SMEM((slots,), i32),
             pltpu.SMEM((slots,), f32),
             pltpu.SMEM((slots,), i32),
@@ -694,22 +680,20 @@
             dma,
             dma((len(pieces(0, chunks)),)),
             dma,
-            dma((len(pieces(0, chunks)),)),
-            dma,
-            dma,
-            dma,
-            dma,
-            dma,
-            dma,
-            dma,
-            dma,
-            dma,
-            dma,
-            dma,
-            dma,
-            dma,
-            dma((2,)),
-            dma((2,)),
+            dma,
+            dma,
+            dma,
+            dma,
+            dma,
+            dma,
+            dma,
+            dma,
+            dma,
+            dma,
+            dma,
+            dma,
+            dma,
+            dma,
         ],
         compiler_params=pltpu.CompilerParams(
             collective_id=0,
@@ -730,7 +714,7 @@
             pltpu.VMEM((slots_dev, shards, LATE * PART, width), f32),
             pltpu.SMEM((slots_dev,), f32),
             pltpu.SMEM((3,), f32),
-            dma((3, slots_dev)),
+            dma((3,)),
         ],
         compiler_params=pltpu.CompilerParams(vmem_limit_bytes=4 * 1024 * 1024),
     )(out, late, total, kinds)

time: 109 us -> 108 us (level)
    pallas_call x1, Pallas kernels: 106 us -> 105 us  [line_step(): pl.pallas_call(functools.partial(line_kernel, blocks, slots_dev), out_sha...]
where the time goes in v5:
time: 108 us
  Pallas kernels  107 us (99%)
    pallas_call x1, Pallas kernels, line_step(): pl.pallas_call(functools.partial(line_kernel, blocks, slots_dev), out_sha...  105 us

profile of v5, /device:TPU:0, one launch (start us, length us, event | category | flops | bytes accessed | tf_op | source)
XLA Modules:
  0.0 107.6 jit_solution(9752930444414027158)
XLA Ops:
  0.6 105.3 %shard_map.58 = (f32[6,8,128,128]{3,2,1,0:T(8,128)S(1)}, bf16[8,5,6,8,128]{4,3,2,1,0:T(8,128)(2,1)S(1)}, f32[1,128]{1,0:T(1,128)S(1)}, s32[1,128]{1,0:T(1,128)S(1)}) custom-call(bf16[64,8,6144]{2,1,0:T(8,128)(2,1)} %bitcast.1, s32[48]{0:T(128)} %joined_hbm.1, s32[48]{0:T(128)} %slot_hbm.1), custom_call_target="tpu_custom_call" | custom-call | tf_op jit(solution)/shard_map/pallas_call | solution.py:635
  105.9 1.7 %shard_map.59 = (f32[6,8,128,128]{3,2,1,0:T(8,128)}, f32[6]{0:T(128)}, f32[3]{0:T(128)}) custom-call(f32[6,8,128,128]{3,2,1,0:T(8,128)S(1)} %get-tuple-element.7.in_ref, bf16[8,5,6,8,128]{4,3,2,1,0:T(8,128)(2,1)S(1)} %get-tuple-element.8.late_ref, f32[1,128]{1,0:T(1,128)S(1)} %get-tuple-element.9.total_ref, s32[1,128]{1,0:T(1,128)S(1)} %get-tuple-element.10.kinds_ref), custom_call_target="tpu_custom_call" | custom-call | tf_op jit(solution)/shard_map/pallas_call | solution.py:704

commit v6 on v5

--- a/solution.py
+++ b/solution.py
@@ -131,6 +131,7 @@
     own_sem,
     far_sem,
     plane_sem,
+    peers_sem,
     beyond_sem,
     r_send,
     r_recv,
@@ -254,13 +255,16 @@
 
     barrier = pltpu.get_barrier_semaphore()
     pl.semaphore_signal(barrier, 1, device_id=(mate, shard), device_id_type=MESH)
-    for o in range(1, 6):
-        pl.semaphore_signal(barrier, 1, device_id=(grp, flip(shard, o)), device_id_type=MESH)
 
     @pl.when(inner)
     def _():
+        for o in range(1, 6):
+            to = (grp, flip(shard, o))
+            pl.semaphore_signal(barrier, 1, device_id=to, device_id_type=MESH)
         pl.semaphore_signal(barrier, 1, device_id=(near, shard), device_id_type=MESH)
         pl.semaphore_wait(barrier, 7)
+        to = (grp, flip(shard, 2))
+        pl.semaphore_signal(plane_sem, 1, device_id=to, device_id_type=MESH)
         own_copy.start()
         pl.semaphore_signal(beyond_sem, 1, device_id=(near, shard), device_id_type=MESH)
         for f in range(2):
@@ -270,7 +274,7 @@
 
     @pl.when(outer)
     def _():
-        pl.semaphore_wait(barrier, 6)
+        pl.semaphore_wait(barrier, 1)
         first_copy.wait()
         done = dict(n=0, f=0, m=LATE)
         for pattern, times in PLAN:
@@ -296,8 +300,6 @@
         own_copy.start()
         late_copy.start()
 
-    pl.semaphore_signal(plane_sem, 1, device_id=(grp, flip(shard, 2)), device_id_type=MESH)
-
     def find(j, carry):
         head = jnp.int32(-1)
         for b in range(blocks):
@@ -313,7 +315,21 @@
         copy.start()
     for copy in index_copies:
         copy.wait()
+
+    @pl.when(inner)
+    def _():
+        pl.semaphore_wait(plane_sem, 1)
+        for o in order:
+            to = (grp, flip(shard, o))
+            pl.semaphore_signal(peers_sem, 1, device_id=to, device_id_type=MESH)
+
     lax.fori_loop(0, slots, find, 0)
+
+    @pl.when(inner)
+    def _():
+        pl.semaphore_wait(peers_sem, shards - 1)
+        pl.semaphore_signal(plane_sem, 1, device_id=(mate, shard), device_id_type=MESH)
+
     own_copy.wait()
 
     def clear(j, carry):
@@ -409,7 +425,6 @@
         for f in range(2):
             far_copy(f).wait()
         pl.semaphore_wait(beyond_sem, 1)
-        pl.semaphore_wait(plane_sem, 1)
         done = dict(n=0, f=0, l=0, m=LATE)
         for pattern, times in PLAN:
             now, per = steps(pattern, done)
@@ -673,6 +688,7 @@
             dma((2,)),
             regular,
             regular,
+            regular,
             dma,
             dma((len(pieces(0, chunks)), 2)),
             dma,

time: 108 us -> 108 us (level)
  no operation moved by 1% of the time
where the time goes in v6:
time: 108 us
  Pallas kernels  107 us (99%)
    pallas_call x1, Pallas kernels, line_step(): pl.pallas_call(functools.partial(line_kernel, blocks, slots_dev), out_sha...  105 us

profile of v6, /device:TPU:0, one launch (start us, length us, event | category | flops | bytes accessed | tf_op | source)
XLA Modules:
  0.0 107.5 jit_solution(6856596283473830961)
XLA Ops:
  0.6 105.2 %shard_map.58 = (f32[6,8,128,128]{3,2,1,0:T(8,128)S(1)}, bf16[8,5,6,8,128]{4,3,2,1,0:T(8,128)(2,1)S(1)}, f32[1,128]{1,0:T(1,128)S(1)}, s32[1,128]{1,0:T(1,128)S(1)}) custom-call(bf16[64,8,6144]{2,1,0:T(8,128)(2,1)} %bitcast.1, s32[48]{0:T(128)} %joined_hbm.1, s32[48]{0:T(128)} %slot_hbm.1), custom_call_target="tpu_custom_call" | custom-call | tf_op jit(solution)/shard_map/pallas_call | solution.py:650
  105.8 1.7 %shard_map.59 = (f32[6,8,128,128]{3,2,1,0:T(8,128)}, f32[6]{0:T(128)}, f32[3]{0:T(128)}) custom-call(f32[6,8,128,128]{3,2,1,0:T(8,128)S(1)} %get-tuple-element.7.in_ref, bf16[8,5,6,8,128]{4,3,2,1,0:T(8,128)(2,1)S(1)} %get-tuple-element.8.late_ref, f32[1,128]{1,0:T(1,128)S(1)} %get-tuple-element.9.total_ref, s32[1,128]{1,0:T(1,128)S(1)} %get-tuple-element.10.kinds_ref), custom_call_target="tpu_custom_call" | custom-call | tf_op jit(solution)/shard_map/pallas_call | solution.py:720
